TPU v7x, 32 devices: a whole 2x2x4 slice. The times are simulated.
32 devices in a mesh: groups: 2 (over y), tp: 4 (over x, core), dp: 4 (over z).
Axes of the slice: x: 2, y: 2, z: 4, core: 2. Of those that a mesh axis runs over, the one named last changes fastest.
Arguments:
- hidden: bfloat16 [128, 2560], P(('groups', 'dp'), 'tp'), parts along dimension 0, may hold values from -40 to 40
- in_gain: float32 [2560], replicated, may hold values from 0.1 to 1.9
- z_weight: bfloat16 [2560, 5120], P(None, 'tp'), may hold values from -0.125 to 0.125
- x_weight: bfloat16 [2560, 5120], P(None, 'tp'), may hold values from -0.125 to 0.125
- bc_weight: bfloat16 [2560, 256], P(None, 'tp'), may hold values from -0.125 to 0.125
- dt_weight: bfloat16 [2560, 80], P(None, 'tp'), may hold values from -0.125 to 0.125
- conv_x_weight: bfloat16 [4, 5120], P(None, 'tp'), may hold values from -3 to 3
- conv_x_bias: bfloat16 [5120], P('tp'), may hold values from -3 to 3
- conv_bc_weight: bfloat16 [4, 256], P(None, 'tp'), may hold values from -3 to 3
- conv_bc_bias: bfloat16 [256], P('tp'), may hold values from -3 to 3
- conv_x_state: bfloat16 [128, 3, 5120], P(('groups', 'dp'), None, 'tp'), parts along dimension 0, may hold values from -6 to 6
- conv_bc_state: bfloat16 [128, 3, 256], P(('groups', 'dp'), None, 'tp'), parts along dimension 0, may hold values from -6 to 6
- dt_bias: float32 [80], P('tp'), may hold values from -4 to -1
- log_rate: float32 [80], P('tp'), may hold values from 0 to 2.5
- skip_gain: float32 [80], P('tp'), may hold values from 0.5 to 2
- ssm_state: float32 [128, 80, 64, 128], P(('groups', 'dp'), 'tp'), parts along dimension 0, may hold values from -20 to 20
- norm_gain: float32 [5120], P('tp'), may hold values from 0.1 to 1.9
- out_weight: bfloat16 [5120, 2560], P('tp'), may hold values from -0.125 to 0.125
- pool_slot: int32 [8, 16], P(('groups', 'dp')), parts along dimension 0, may hold values from 0 to 15, as said below
- active: int32 [128], P(('groups', 'dp')), parts along dimension 0, may hold values 0 or 1
Outputs:
- layer_out: bfloat16 [128, 2560], P(('groups', 'dp'), 'tp'), parts along dimension 0
- conv_x_next: bfloat16 [128, 3, 5120], P(('groups', 'dp'), None, 'tp'), parts along dimension 0
- conv_bc_next: bfloat16 [128, 3, 256], P(('groups', 'dp'), None, 'tp'), parts along dimension 0
- ssm_next: float32 [128, 80, 64, 128], P(('groups', 'dp'), 'tp'), parts along dimension 0
There are 2 independent parts, one for each index of `groups`. A program takes and returns all parts, laid end to end along the dimension named above; an argument that names none is the same for every part. Nothing has to cross between parts.
Inputs may be any that keep to these rules, and one draw needn't show every extreme that they name: `pool_slot`: each row is a permutation of 0 to 15.
All inputs are finite; a program needn't handle non-finite values. No bound on the sum of `active` on one device may be relied on, other than what follows from the above.
Results may differ from a plain program's by a relative error of at most 0.0085.
Values may be sent and summed in bfloat16 or wider, within the bound.
No kernel may reach another device: no remote copies, remote signals or barrier semaphores. Data moves between devices by JAX's collectives and lax.ppermute only.
A program may use at most 128 MiB of HBM per device.

v0:
```python
import jax
import jax.numpy as jnp
from jax import lax
from jax.sharding import PartitionSpec as P

HP = 64
NS = 128
INNER = 5120


def convolve(old_state, current, weight, conv_bias):
    window = jnp.concatenate(
        [old_state.astype(jnp.float32), current.astype(jnp.float32)[:, None, :]], axis=1
    )
    conv_out = jnp.sum(window * weight.astype(jnp.float32)[None], axis=1) + conv_bias.astype(
        jnp.float32
    )
    return (jax.nn.silu(conv_out).astype(jnp.bfloat16), window[:, 1:, :].astype(jnp.bfloat16))


def shards(
    hidden,
    in_gain,
    z_weight,
    x_weight,
    bc_weight,
    dt_weight,
    conv_x_weight,
    conv_x_bias,
    conv_bc_weight,
    conv_bc_bias,
    conv_x_state,
    conv_bc_state,
    dt_bias,
    log_rate,
    skip_gain,
    ssm_state,
    norm_gain,
    out_weight,
    pool_slot,
    active,
):
    seq_rows = hidden.shape[0]
    hidden_f32 = hidden.astype(jnp.float32)
    owner_slot = pool_slot.reshape(-1)
    requests = jnp.arange(seq_rows, dtype=jnp.int32)
    onehot = owner_slot[:, None] == requests[None, :]
    at_slot = jnp.sum(jnp.where(onehot, requests[:, None], 0), axis=0)
    bc_matrix, bc_taps, bc_shift, bc_old = (bc_weight, conv_bc_weight, conv_bc_bias, conv_bc_state)
    matrices = (z_weight, x_weight, bc_matrix, dt_weight)
    whole_rows = lax.all_gather(hidden, "tp", axis=1, tiled=True).astype(jnp.float32)
    inv_rms = lax.rsqrt(jnp.mean(whole_rows * whole_rows, axis=1, keepdims=True) + 1e-05)
    normed = (whole_rows * inv_rms * in_gain).astype(jnp.bfloat16)
    proj_sums = tuple(
        (jnp.dot(normed, matrix, preferred_element_type=jnp.float32) for matrix in matrices)
    )
    z_proj, x_proj, bc_proj, dt_proj = (part_sum.astype(jnp.bfloat16) for part_sum in proj_sums)
    is_live = active[at_slot] > 0
    x_conv, x_kept = convolve(conv_x_state, x_proj[at_slot], conv_x_weight, conv_x_bias)
    conv_x_next = jnp.where(is_live[:, None, None], x_kept, conv_x_state)
    bc_conv, bc_kept = convolve(bc_old, bc_proj[at_slot], bc_taps, bc_shift)
    bc_full = lax.all_gather(bc_conv, "tp", axis=1, tiled=True)
    conv_bc_next = jnp.where(is_live[:, None, None], bc_kept, conv_bc_state)
    b_rows = bc_full[:, :NS].astype(jnp.float32)
    c_rows = bc_full[:, NS:].astype(jnp.float32)
    dt_step = jax.nn.softplus(dt_proj[at_slot].astype(jnp.float32) + dt_bias)
    decay_rate = jnp.exp(-dt_step * jnp.exp(log_rate))
    heads_dev = ssm_state.shape[1]
    x_heads = x_conv.astype(jnp.float32).reshape(seq_rows, heads_dev, HP)
    fresh_state = (
        decay_rate[:, :, None, None] * ssm_state
        + (dt_step[:, :, None] * x_heads)[:, :, :, None] * b_rows[:, None, None, :]
    )
    fresh_state = jnp.where(is_live[:, None, None, None], fresh_state, ssm_state)
    y_slot = (
        jnp.einsum("bhpn,bn->bhp", fresh_state, c_rows, precision=lax.Precision.HIGHEST)
        + skip_gain[None, :, None] * x_heads
    )
    y_request = y_slot.reshape(seq_rows, heads_dev * HP)[owner_slot]
    gated_y = y_request * jax.nn.silu(z_proj.astype(jnp.float32))
    part_sq = jnp.sum(gated_y * gated_y, axis=1)
    scaled = (gated_y * norm_gain).astype(jnp.bfloat16)
    branch_part = jnp.dot(scaled, out_weight, preferred_element_type=jnp.float32)
    sq_total = lax.psum(part_sq, "tp")
    branch_sum = lax.psum_scatter(branch_part, "tp", scatter_dimension=1, tiled=True)
    inv_out = lax.rsqrt(sq_total / INNER + 1e-05)
    live_request = active > 0
    layer_out = jnp.where(
        live_request[:, None],
        (hidden_f32 + inv_out[:, None] * branch_sum).astype(jnp.bfloat16),
        hidden,
    )
    return (layer_out, conv_x_next, conv_bc_next, fresh_state)


def solution(mesh):
    placed = (
        P(("groups", "dp"), "tp"),
        P(),
        P(None, "tp"),
        P(None, "tp"),
        P(None, "tp"),
        P(None, "tp"),
        P(None, "tp"),
        P("tp"),
        P(None, "tp"),
        P("tp"),
        P(("groups", "dp"), None, "tp"),
        P(("groups", "dp"), None, "tp"),
        P("tp"),
        P("tp"),
        P("tp"),
        P(("groups", "dp"), "tp", None, None),
        P("tp"),
        P("tp", None),
        P(("groups", "dp"), None),
        P(("groups", "dp")),
    )
    return jax.shard_map(
        shards,
        mesh=mesh,
        in_specs=placed,
        out_specs=(
            P(("groups", "dp"), "tp"),
            P(("groups", "dp"), None, "tp"),
            P(("groups", "dp"), None, "tp"),
            P(("groups", "dp"), "tp", None, None),
        ),
        check_vma=False,
    )
```

profile of v0, /device:TPU:0, one launch (start us, length us, event | category | flops | bytes accessed | tf_op | source)
XLA Modules:
  0.0 99.4 jit_solution(2938641339145012871)
XLA Ops:
  7.2 6.6 %all_gather.6 = bf16[16,2560]{1,0:T(8,128)(2,1)S(1)} all-gather(bf16[16,640]{1,0:T(8,128)(2,1)} %param.20), channel_id=1, replica_groups=mesh['groups'=2,'tp'=4,'dp'=4] {'tp'}, dimensions={1}, use_global_device_ids=true | all-gather | bytes 102400 | tf_op jit(solution)/shard_map/all_gather | solution.py:51
  14.0 0.7 fusion.16
  14.7 0.7 select_reduce_fusion
  15.4 0.7 convert_element_type.107
  16.1 3.9 %convolution_convert_fusion.1 = bf16[16,1280]{1,0:T(8,128)(2,1)S(1)} fusion(bf16[2560,1280]{1,0:T(8,128)(2,1)} %param.23, bf16[16,2560]{1,0:T(8,128)(2,1)S(1)} %all_gather.6, f32[2560]{0:T(1024)} %param.21, f32[16]{0:T(128)S(1)} %add_rsqrt_fusion.1), kind=kOutput, calls=%fused_computation.8 | convolution fusion | flops 105041920 | bytes 6686784 | tf_op jit(solution)/shard_map/dot_general | solution.py:55
  20.6 0.9 multiply_reduce_fusion
  21.7 1.1 %convolution_convert_fusion.2 = bf16[16,20]{1,0:T(8,128)(2,1)S(1)} fusion(bf16[2560,20]{0,1:T(8,128)(2,1)} %param.25, bf16[16,2560]{1,0:T(8,128)(2,1)S(1)} %all_gather.6, f32[2560]{0:T(1024)} %param.21, f32[16]{0:T(128)S(1)} %add_rsqrt_fusion.1), kind=kOutput, calls=%fused_computation.9 | convolution fusion | flops 1802560 | bytes 195264 | tf_op jit(solution)/shard_map/dot_general | solution.py:55
  24.0 0.8 reshape.182
  24.8 0.9 convolution_convert_fusion.3
  26.4 0.7 convert_element_type.112
  27.7 0.7 multiply_reduce_fusion.2
  28.4 5.5 %all-gather = bf16[4,64,16]{1,2,0:T(8,128)(2,1)S(1)} all-gather(bf16[1,64,16]{1,2,0:T(8,128)(2,1)S(1)} %fusion.14), channel_id=1, replica_groups=mesh['groups'=2,'tp'=4,'dp'=4] {'tp'}, dimensions={0}, use_global_device_ids=true | all-gather | bytes 10240 | tf_op jit(solution)/shard_map/all_gather | solution.py:62
  34.0 1.3 %gather_fusion = s32[16]{0:T(128)S(1)} fusion(s32[16]{0:T(128)} %param.39, s32[1024]{0:T(1024)S(1)} %pad_clamp_fusion.1), kind=kCustom, calls=%fused_computation | custom fusion | bytes 192 | tf_op jit(solution)/shard_map/gather | solution.py:58
  35.3 0.7 multiply_exponential_fusion
  36.1 8.0 %add_select_fusion = f32[16,20,64,128]{3,2,1,0:T(8,128)S(1)} fusion(f32[16,20,64,128]{3,2,1,0:T(8,128)} %param.35, f32[16,128]{1,0:T(8,128)S(1)} %get-tuple-element.5, f32[16,20,64]{2,1,0:T(8,128)S(1)} %convert_multiply_fusion.1, f32[16,20]{1,0:T(8,128)S(1)} %get-tuple-element.6, pred[16]{0:T(512)(128)(4,1)S(1)} %broadcast_compare_fusion), kind=kLoop, calls=%fused_computation.5 | loop fusion | flops 10485760 | bytes 21062928 | tf_op jit(solution)/shard_map/jit(_where)/select_n | solution.py:74
  44.2 4.0 %copy-done.2 = f32[16,20,64,128]{3,2,1,0:T(8,128)} copy-done((f32[16,20,64,128]{3,2,1,0:T(8,128)}, f32[16,20,64,128]{3,2,1,0:T(8,128)S(1)}, u32[]{:S(2)}) %copy-start.2) | copy-done | bytes 10485784
  48.2 12.2 %fusion.12 = f32[16,1,20,64]{3,1,2,0:T(1,128)S(1)} fusion(f32[16,20,64,128]{3,2,1,0:T(8,128)S(1)} %add_select_fusion, bf16[16,128,1,1]{1,0,2,3:T(8,128)(2,1)S(1)} %get-tuple-element.4), kind=kOutput, calls=%fused_computation.40 | convolution fusion | flops 31457280 | bytes 10571776 | tf_op jit(solution)/shard_map/bhpn,bn->bhp/dot_general | solution.py:76
  61.3 4.0 %multiply_reduce_fusion.1 = (f32[16]{0:T(128)S(1)}, f32[16,1280]{1,0:T(8,128)S(1)}) fusion(f32[16,1280]{1,0:T(8,128)S(1)} %gather_fusion.4, bf16[2560,1280]{1,0:T(8,128)(2,1)} %param.22, bf16[16,2560]{1,0:T(8,128)(2,1)S(1)} %all_gather.6, f32[2560]{0:T(1024)S(1)} %copy-done.4, f32[16]{0:T(128)S(1)} %add_rsqrt_fusion.1), kind=kOutput, calls=%fused_computation.27 | convolution fusion | flops 105205744 | bytes 6809728 | tf_op jit(solution)/shard_map/dot_general | solution.py:55
  65.3 4.5 %fusion.7 = f32[16,2560]{1,0:T(8,128)} fusion(bf16[1280,2560]{1,0:T(8,128)(2,1)} %param.37, f32[16,1280]{1,0:T(8,128)S(1)} %get-tuple-element.9, f32[1280]{0:T(1024)S(1)} %copy-done.7), kind=kOutput, calls=%fused_computation.29 | convolution fusion | flops 104898560 | bytes 6804480 | tf_op jit(solution)/shard_map/dot_general | solution.py:83
  69.8 0.7 fusion.6
  70.6 7.3 %psum.7 = f32[16]{0:T(128)S(1)} all-reduce(f32[16]{0:T(128)S(1)} %get-tuple-element.8), channel_id=1, replica_groups=mesh['groups'=2,'tp'=4,'dp'=4] {'tp'}, use_global_device_ids=true, to_apply=%region_5.6 | all-reduce | flops 16 | bytes 128 | tf_op jit(solution)/shard_map/psum | solution.py:84
  77.9 0.7 fusion.11
  78.5 12.6 %reduce-scatter.2.cloned.1.call-done = f32[16,640]{1,0:T(8,128)} async-done(((f32[16,2560]{1,0:T(8,128)}), f32[16,640]{1,0:T(8,128)}) %reduce-scatter.2.cloned.1.call-update) | async-done | bytes 40976 | tf_op jit(solution)/shard_map/reduce_scatter | solution.py:85
  91.1 1.5 %fusion.9 = bf16[16,640]{1,0:T(8,128)(2,1)} fusion(bf16[16,640]{1,0:T(8,128)(2,1)S(1)} %copy-done.5, f32[16,640]{1,0:T(8,128)} %reduce-scatter.2.cloned.1.call-done, f32[16]{0:T(128)S(1)} %add_rsqrt_fusion, pred[16]{0:T(512)(128)(4,1)S(1)} %broadcast_compare_fusion.1), kind=kLoop, calls=%fused_computation.33 | loop fusion | flops 51200 | bytes 82000 | tf_op jit(solution)/shard_map/jit(_where)/select_n | solution.py:88
  (41 shorter events, 4.5 us)
Async XLA Ops:
  7.2 17.6 %copy-start = (bf16[2560,64]{0,1:T(8,128)(2,1)S(1)}, bf16[2560,64]{0,1:T(8,128)(2,1)}, u32[]{:S(2)}) copy-start(bf16[2560,64]{0,1:T(8,128)(2,1)} %param.24) | copy-start | bytes 983044
  7.2 84.0 %reduce-scatter.2.cloned.1.call-start = ((), (), s32[]{:S(2)}) async-start(), calls=%async_computation.1 | async-start | bytes 204800 | tf_op jit(solution)/shard_map/reduce_scatter | solution.py:85
  44.1 4.1 %copy-start.2 = (f32[16,20,64,128]{3,2,1,0:T(8,128)}, f32[16,20,64,128]{3,2,1,0:T(8,128)S(1)}, u32[]{:S(2)}) copy-start(f32[16,20,64,128]{3,2,1,0:T(8,128)S(1)} %add_select_fusion) | copy-start | bytes 31457284
  44.1 16.3 %copy-start.8 = (f32[20]{0:T(128)S(1)}, f32[20]{0:T(128)}, u32[]{:S(2)}) copy-start(f32[20]{0:T(128)} %param.34) | copy-start | bytes 244
  44.2 17.1 %copy-start.4 = (f32[2560]{0:T(1024)S(1)}, f32[2560]{0:T(1024)}, u32[]{:S(2)}) copy-start(f32[2560]{0:T(1024)} %param.21) | copy-start | bytes 30724
  44.2 21.1 %copy-start.7 = (f32[1280]{0:T(1024)S(1)}, f32[1280]{0:T(1024)}, u32[]{:S(2)}) copy-start(f32[1280]{0:T(1024)} %param.36) | copy-start | bytes 15364
  48.2 21.6 %copy-start.1 = (s32[16]{0:T(128)S(1)}, s32[16]{0:T(128)}, u32[]{:S(2)}) copy-start(s32[16]{0:T(128)} %param.39) | copy-start | bytes 196
  48.2 21.6 %copy-start.3 = (bf16[16,3,1280]{2,0,1:T(8,128)(2,1)S(1)}, bf16[16,3,1280]{2,0,1:T(8,128)(2,1)}, u32[]{:S(2)}) copy-start(bf16[16,3,1280]{2,0,1:T(8,128)(2,1)} %param.30) | copy-start | bytes 368644
  60.5 17.4 %copy-start.6 = (bf16[16,3,64]{2,0,1:T(8,128)(2,1)S(1)}, bf16[16,3,64]{2,0,1:T(8,128)(2,1)}, u32[]{:S(2)}) copy-start(bf16[16,3,64]{2,0,1:T(8,128)(2,1)} %param.31) | copy-start | bytes 18436
  60.5 30.7 %copy-start.5 = (bf16[16,640]{1,0:T(8,128)(2,1)S(1)}, bf16[16,640]{1,0:T(8,128)(2,1)}, u32[]{:S(2)}) copy-start(bf16[16,640]{1,0:T(8,128)(2,1)} %param.20) | copy-start | bytes 61444
Sparse Core Ops, SparseCore 0:
  69.9 21.1 reduce-scatter.1
where the time goes:
time: 100 us; the launch traced here: 99.4 us
  matrix products  26.7 us (27%)
  blocking collectives  19.4 us (19%)
  other arithmetic  17.1 us (17%)
  between operations  14.2 us (14%)
  waiting for transfers between devices  12.6 us (13%)
  local copies, waits for them, and re-layouts  9.51 us (10%)
    reduce_scatter x1, waiting for transfers between devices, shards(): lax.psum_scatter(branch_part, 'tp', scatter_dimension=1, tiled=True)  12.6 us
    dot_general x1, matrix products, shards(): jnp.einsum('bhpn,bn->bhp', fresh_state, c_rows, precision=lax.Precision.H...  12.2 us
    dot_general x4, matrix products, shards(): jnp.dot(normed, matrix, preferred_element_type=jnp.float32)  9.94 us
    select_n x1, other arithmetic, shards(): jnp.where(is_live[:, None, None, None], fresh_state, ssm_state)  7.99 us
    psum x1, blocking collectives, shards(): sq_total = lax.psum(part_sq, 'tp')  7.27 us
    all_gather x1, blocking collectives, shards(): lax.all_gather(hidden, 'tp', axis=1, tiled=True).astype(jnp.float32)  6.63 us
    all_gather x1, blocking collectives, shards(): bc_full = lax.all_gather(bc_conv, 'tp', axis=1, tiled=True)  5.46 us
    dot_general x1, matrix products, shards(): jnp.dot(scaled, out_weight, preferred_element_type=jnp.float32)  4.48 us
  transfers between devices with their start and end apart: 1, of which 1 were waited for; matrix products, arithmetic and copies ran while one was open for 1% of the time, Pallas kernels for 0%

commit v1 on v0

v1 whole, which is shorter than its diff:
```python
import functools
import jax
import jax.numpy as jnp
from jax import lax
from jax.experimental import pallas as pl
from jax.experimental.pallas import tpu as pltpu
from jax.sharding import PartitionSpec as P

F32 = jnp.float32
BF16 = jnp.bfloat16
NT = (((1,), (1,)), ((), ()))
TN = (((0,), (0,)), ((), ()))
EPS = 1e-05


def column(row):
    n = row.shape[1]
    eye = lax.broadcasted_iota(jnp.int32, (n, n), 0) == lax.broadcasted_iota(jnp.int32, (n, n), 1)
    return jnp.sum(jnp.where(eye, jnp.broadcast_to(row, (n, n)), jnp.zeros((), row.dtype)), axis=1, keepdims=True)


def silu(v):
    return v * (1.0 / (1.0 + jnp.exp(-v)))


def softplus(v):
    return jnp.maximum(v, 0.0) + jnp.log1p(jnp.exp(-jnp.abs(v)))


def owner_mask(slot_row):
    n = slot_row.shape[1]
    slot_col = column(slot_row.astype(F32))
    return slot_col == lax.broadcasted_iota(jnp.int32, (n, n), 1).astype(F32)


def taps(old, current, weight, bias):
    acc = old[0] * weight[0:1]
    acc = acc + old[1] * weight[1:2]
    acc = acc + old[2] * weight[2:3]
    acc = acc + current * weight[3:4]
    return silu(acc + bias).astype(BF16)


def shift_state(st_ref, newest, live_own, next_ref):
    live_slot = lax.dot_general(live_own, jnp.ones(newest.shape, BF16), TN, preferred_element_type=F32) > 0.5
    at_slot = lax.dot_general(live_own, newest, TN, preferred_element_type=F32)
    for k in range(3):
        newer = st_ref[k + 1].astype(F32) if k < 2 else at_slot
        next_ref[k] = jnp.where(live_slot, newer, st_ref[k].astype(F32)).astype(BF16)


def prep_kernel(count, *refs):
    src, refs = refs[:count], refs[count:]
    (gain_ref, ngain_ref, own_ref, live_own_ref, bcw_ref, dtw_ref, bcst_ref, bcbase_ref, bctap_ref, xst_ref,
     xbase_ref, xtap_ref, dtb_ref, rate_ref, skip_ref, hid_ref, live_ref) = refs[:17]
    slot_s, act_s, bccw_s, bccb_s, xcw_s, xcb_s, sems = refs[17:]
    dst = (gain_ref, ngain_ref, slot_s, act_s, bcw_ref, dtw_ref, bcst_ref, bccw_s, bccb_s, xst_ref, xcw_s, xcb_s,
           dtb_ref, rate_ref, skip_ref, hid_ref)
    copies = [pltpu.make_async_copy(a, b, sems.at[i]) for i, (a, b) in enumerate(zip(src, dst))]
    order = (2, 3, 6, 7, 8, 9, 10, 11, 4, 5, 0, 1, 12, 13, 14, 15)
    for i in order:
        copies[i].start()
    copies[2].wait()
    copies[3].wait()
    own = owner_mask(slot_s[...])
    live = column(act_s[...].astype(F32)) > 0.0
    own_b = own.astype(BF16)
    own_ref[...] = own.astype(F32)
    live_own_ref[...] = (own & live).astype(BF16)
    live_ref[...] = jnp.broadcast_to(live.astype(F32), live_ref.shape)
    for st, cw, cb, base, tap, waits in ((bcst_ref, bccw_s, bccb_s, bcbase_ref, bctap_ref, (6, 7, 8)),
                                         (xst_ref, xcw_s, xcb_s, xbase_ref, xtap_ref, (9, 10, 11))):
        for i in waits:
            copies[i].wait()
        weight = cw[...].astype(F32)
        acc = jnp.broadcast_to(cb[...].astype(F32), base.shape)
        for k in range(3):
            acc = acc + jnp.dot(own_b, st[k], preferred_element_type=F32) * weight[k:k + 1]
        base[...] = acc
        tap[...] = weight[3:4]
    for i in (4, 5, 0, 1, 12, 13, 14, 15):
        copies[i].wait()


def bc_kernel(n, *refs):
    parts, refs = refs[:n], refs[n:]
    gain_ref, own_ref, w_ref, base_ref, tap_ref, normed_ref, bc_ref, proj_ref = refs
    me = lax.axis_index("tp")
    blocks = [p[...] for p in parts]
    width = blocks[0].shape[1]
    for s in range(n):
        pick = blocks[0]
        for k in range(1, n):
            pick = jnp.where(lax.rem(me - k + n, n) == s, blocks[k], pick)
        normed_ref[:, s * width:(s + 1) * width] = pick
    rows = normed_ref[...].astype(F32)
    inv = lax.rsqrt(jnp.mean(rows * rows, axis=1, keepdims=True) + EPS)
    normed = (rows * inv * gain_ref[...]).astype(BF16)
    normed_ref[...] = normed
    proj = lax.dot_general(normed, w_ref[...], NT, preferred_element_type=F32).astype(BF16)
    proj_ref[...] = proj
    bc_ref[...] = silu(base_ref[...] + tap_ref[...] * proj.astype(F32)).astype(BF16)


def in_kernel(hp, normed_ref, xw_ref, zw_ref, dtw_ref, base_ref, tap_ref, dtb_ref, rate_ref, skip_ref, own_ref,
              live_ref, xproj_ref, g1_ref, g2_ref, g3_ref, u_ref, dec_ref):
    normed = normed_ref[...]
    seqs = normed.shape[0]
    chans = xw_ref.shape[1]
    heads = dtw_ref.shape[0]
    live = live_ref[:, :1] > 0.0
    dt = lax.dot_general(normed, dtw_ref[...], NT, preferred_element_type=F32).astype(BF16).astype(F32)
    dt = softplus(dt + dtb_ref[...])
    decay = jnp.exp(-dt * jnp.exp(rate_ref[...]))
    spread = (lax.broadcasted_iota(jnp.int32, (heads, chans), 1) // hp
              == lax.broadcasted_iota(jnp.int32, (heads, chans), 0)).astype(F32)
    wide = jnp.concatenate([dt, decay, jnp.broadcast_to(skip_ref[...], dt.shape)], axis=0)
    wide = jnp.dot(wide, spread, preferred_element_type=F32, precision=lax.Precision.HIGHEST)
    dt_w, dec_w, skip_w = wide[:seqs], wide[seqs:2 * seqs], wide[2 * seqs:]
    kept = jnp.where(live, decay, 1.0)
    kept_slot = lax.dot_general(kept, own_ref[...], TN, preferred_element_type=F32, precision=lax.Precision.HIGHEST)
    for s in range(seqs):
        dec_ref[s] = jnp.broadcast_to(kept_slot[:, s:s + 1], (heads, dec_ref.shape[2]))
    xproj = jnp.dot(normed, xw_ref[...], preferred_element_type=F32).astype(BF16)
    xproj_ref[...] = xproj
    x = silu(base_ref[...] + tap_ref[...] * xproj.astype(F32)).astype(BF16).astype(F32)
    u = dt_w * x
    zproj = jnp.dot(normed, zw_ref[...], preferred_element_type=F32).astype(BF16)
    gate = silu(zproj.astype(F32))
    g1_ref[...] = gate * dec_w
    g2_ref[...] = gate * u
    g3_ref[...] = gate * (skip_w * x)
    u = jnp.where(live, u, 0.0)
    high = u.astype(BF16)
    u_ref[:seqs] = high
    u_ref[seqs:] = (u - high.astype(F32)).astype(BF16)


def out_kernel(n, *refs):
    parts, refs = refs[:n], refs[n:]
    state_ref, own_ref, g1_ref, g2_ref, g3_ref, gain_ref, w_ref = refs[:7]
    sends, (own_sum_ref, bcf_ref, stage) = refs[7:7 + n - 1], refs[7 + n - 1:]
    me = lax.axis_index("tp")
    seqs = g1_ref.shape[0]
    ns = state_ref.shape[2]
    blocks = [p[...] for p in parts]
    width = blocks[0].shape[1]
    for s in range(n):
        pick = blocks[0]
        for k in range(1, n):
            pick = jnp.where(lax.rem(me - k + n, n) == s, blocks[k], pick)
        bcf_ref[:, s * width:(s + 1) * width] = pick
    own = own_ref[...] > 0.5
    b_rows, c_rows = bcf_ref[:, :ns].astype(F32), bcf_ref[:, ns:].astype(F32)
    dot_bc = jnp.sum(b_rows * c_rows, axis=1, keepdims=True)
    y = None
    for s in range(0, seqs, 2):
        pair = [jnp.where(own[:, t:t + 1], c_rows, 0.0).astype(BF16) for t in (s, s + 1)]
        both = jnp.concatenate([state_ref[s].astype(BF16), state_ref[s + 1].astype(BF16)], axis=1)
        term = lax.dot_general(jnp.concatenate(pair, axis=1), both, NT, preferred_element_type=F32)
        y = term if y is None else y + term
    gated = g1_ref[...] * y + g2_ref[...] * dot_bc + g3_ref[...]
    part_sq = jnp.sum(gated * gated, axis=1, keepdims=True)
    scaled = (gated * gain_ref[...]).astype(BF16)
    sq_high = part_sq.astype(BF16).astype(F32)
    width = w_ref.shape[1] // n
    lane = lax.broadcasted_iota(jnp.int32, (seqs, 128), 1)
    tail = jnp.where(lane == 0, sq_high, jnp.where(lane == 1, part_sq - sq_high, 0.0))
    for d in range(n):
        stage[d, :, :width] = jnp.dot(scaled, w_ref[:, d * width:(d + 1) * width], preferred_element_type=F32)
        stage[d, :, width:] = tail
    own_sum_ref[...] = stage[me]
    for k in range(1, n):
        sends[k - 1][...] = stage[lax.rem(me + k, n)].astype(BF16)


def state_kernel(state_ref, u_ref, dec_ref, bcf_ref, own_ref, live_own_ref, xst_ref, xproj_ref, bcst_ref, bcproj_ref,
                 next_ref, xnext_ref, bcnext_ref, ring, sems):
    seqs, chans, ns = state_ref.shape
    heads = dec_ref.shape[1]
    hp = chans // heads
    own = own_ref[...] > 0.5
    b_rows = bcf_ref[:, :ns].astype(F32)
    u_rows = u_ref[...]
    depth = ring.shape[0]

    def copy(s):
        return pltpu.make_async_copy(ring.at[s // 2 % depth], next_ref.at[pl.ds(s, 2)], sems.at[s // 2 % depth])

    for s in range(0, seqs, 2):
        pair = jnp.concatenate([jnp.where(own[:, t:t + 1], b_rows, 0.0).astype(BF16) for t in (s, s + 1)], axis=1)
        fresh = lax.dot_general(u_rows, jnp.concatenate([pair, pair], axis=0), TN, preferred_element_type=F32)
        if s // 2 >= depth:
            copy(s - 2 * depth).wait()
        for t in range(2):
            for h in range(heads):
                rows = slice(h * hp, (h + 1) * hp)
                ring[s // 2 % depth, t, rows, :] = (
                    state_ref[s + t, rows, :] * dec_ref[s + t, h:h + 1, :] + fresh[rows, t * ns:(t + 1) * ns]
                )
        copy(s).start()
    shift_state(xst_ref, xproj_ref[...], live_own_ref[...], xnext_ref)
    shift_state(bcst_ref, bcproj_ref[...], live_own_ref[...], bcnext_ref)
    for s in range(max(0, seqs - 2 * depth), seqs, 2):
        copy(s).wait()


def final_kernel(chans, hid_ref, live_ref, own_ref, *refs):
    got, out_ref = refs[:-1], refs[-1]
    width = hid_ref.shape[1]
    total = own_ref[...]
    for g in got:
        total = total + g[...].astype(F32)
    sq = total[:, width:width + 1] + total[:, width + 1:width + 2]
    inv_out = lax.rsqrt(sq / chans + EPS)
    hidden = hid_ref[...]
    out = (hidden.astype(F32) + inv_out * total[:, :width]).astype(BF16)
    out_ref[...] = jnp.where(live_ref[:, :1] > 0.0, out, hidden)


VM = pl.BlockSpec(memory_space=pltpu.VMEM)
HB = pl.BlockSpec(memory_space=pltpu.HBM)


def call(kernel, name, out, ins, args, outs=None, scratch=(), flops=1e6, moved=1e5, mib=4):
    return pl.pallas_call(
        kernel,
        out_shape=out,
        in_specs=ins,
        out_specs=tuple(outs or [VM] * len(out)),
        scratch_shapes=list(scratch),
        name=name,
        compiler_params=pltpu.CompilerParams(vmem_limit_bytes=mib * 2 ** 20),
        cost_estimate=pl.CostEstimate(flops=int(flops), bytes_accessed=int(moved), transcendentals=0),
    )(*args)


def spread_out(values, n):
    return [lax.ppermute(v, "tp", [(i, (i + k) % n) for i in range(n)]) for k, v in enumerate(values, 1)]


def shards(hidden, in_gain, z_weight, x_weight, bc_weight, dt_weight, conv_x_weight, conv_x_bias, conv_bc_weight,
           conv_bc_bias, conv_x_state, conv_bc_state, dt_bias, log_rate, skip_gain, ssm_state, norm_gain, out_weight,
           pool_slot, active, *, n):
    seqs, heads, hp, ns = ssm_state.shape
    chans = heads * hp
    width = hidden.shape[1]
    bcw = bc_weight.shape[1]
    row = lambda v: v.reshape(1, -1)
    sds = jax.ShapeDtypeStruct
    like = lambda v: sds(v.shape, v.dtype)
    state = ssm_state.reshape(seqs, chans, ns)
    parts = [hidden] + spread_out([hidden] * (n - 1), n)
    src = tuple(pltpu.with_memory_space_constraint(v, pltpu.HBM) for v in (row(in_gain), row(norm_gain), pool_slot.reshape(1, -1), row(active), bc_weight.T, dt_weight.T,
           conv_bc_state.transpose(1, 0, 2), conv_bc_weight, row(conv_bc_bias), conv_x_state.transpose(1, 0, 2),
           conv_x_weight, row(conv_x_bias), row(dt_bias), row(log_rate), row(skip_gain), hidden))
    held = {i: pltpu.VMEM(src[i].shape, src[i].dtype) for i in (2, 3, 7, 8, 10, 11)}
    (gain, ngain, own, live_own, bcw_v, dtw_v, bcst, bcbase, bctap, xst, xbase, xtap, dtb, rate, skip, hid, live) = call(
        functools.partial(prep_kernel, len(src)), "prep",
        (like(src[0]), like(src[1]), sds((seqs, seqs), F32), sds((seqs, seqs), BF16), like(src[4]), like(src[5]),
         like(src[6]), sds((seqs, bcw), F32), sds((1, bcw), F32), like(src[9]), sds((seqs, chans), F32),
         sds((1, chans), F32), like(src[12]), like(src[13]), like(src[14]), like(hidden), sds((seqs, 128), F32)),
        [HB] * len(src), src, scratch=[*held.values(), pltpu.SemaphoreType.DMA((len(src),))], flops=4e6, moved=16e6)
    normed, bc_own, bcproj = call(
        functools.partial(bc_kernel, n), "bc",
        (sds((seqs, n * width), BF16), sds((seqs, bcw), BF16), sds((seqs, bcw), BF16)),
        [VM] * (n + 5), (*parts, gain, own, bcw_v, bcbase, bctap), flops=4e6)
    bc_parts = [bc_own] + spread_out([bc_own] * (n - 1), n)
    wide = sds((seqs, chans), F32)
    xproj, g1, g2, g3, u, dec = call(
        functools.partial(in_kernel, hp), "proj",
        (sds((seqs, chans), BF16), wide, wide, wide, sds((2 * seqs, chans), BF16), sds((seqs, heads, 128), F32)),
        [VM] * 11, (normed, x_weight, z_weight, dtw_v, xbase, xtap, dtb, rate, skip, own, live), flops=2e8, moved=14e6)
    *sends, own_sum, bcf = call(
        functools.partial(out_kernel, n), "out",
        (*[sds((seqs, width + 128), BF16)] * (n - 1), sds((seqs, width + 128), F32), sds((seqs, n * bcw), BF16)),
        [VM] * (n + 7), (*bc_parts, state, own, g1, g2, g3, ngain, out_weight),
        scratch=[pltpu.VMEM((n, seqs, width + 128), F32)], flops=2e8, moved=14e6, mib=12)
    got = spread_out(sends, n)
    fresh, x_next, bc_next = call(
        state_kernel, "state", (like(state), like(xst), like(bcst)), [VM] * 10,
        (state, u, dec, bcf, own, live_own, xst, xproj, bcst, bcproj), outs=(HB, VM, VM),
        scratch=[pltpu.VMEM((4, 2, chans, ns), F32), pltpu.SemaphoreType.DMA((4,))], flops=2e8, moved=14e6, mib=12)
    layer_out, = call(functools.partial(final_kernel, chans * n), "final", (like(hidden),), [VM] * (n + 2),
                      (hid, live, own_sum, *got))
    return (layer_out, x_next.transpose(1, 0, 2), bc_next.transpose(1, 0, 2), fresh.reshape(ssm_state.shape))


def solution(mesh):
    placed = (
        P(("groups", "dp"), "tp"), P(), P(None, "tp"), P(None, "tp"), P(None, "tp"), P(None, "tp"), P(None, "tp"),
        P("tp"), P(None, "tp"), P("tp"), P(("groups", "dp"), None, "tp"), P(("groups", "dp"), None, "tp"), P("tp"),
        P("tp"), P("tp"), P(("groups", "dp"), "tp", None, None), P("tp"), P("tp", None), P(("groups", "dp"), None),
        P(("groups", "dp")),
    )
    return jax.shard_map(
        functools.partial(shards, n=mesh.shape["tp"]),
        mesh=mesh,
        in_specs=placed,
        out_specs=(P(("groups", "dp"), "tp"), P(("groups", "dp"), None, "tp"), P(("groups", "dp"), None, "tp"),
                   P(("groups", "dp"), "tp", None, None)),
        check_vma=False,
    )
```

time: 100 us -> 37.8 us (0.38)
  matrix products: 26.7 us -> 0 us
  blocking collectives: 19.4 us -> 0 us
  other arithmetic: 17.1 us -> 0 us
  between operations: 14.2 us -> 0.76 us
  Pallas kernels: 0 us -> 13.2 us
  waiting for transfers between devices: 12.6 us -> 0.02 us
  starting transfers between devices: 0.04 us -> 8.6 us
  local copies, waits for them, and re-layouts: 9.51 us -> 14.8 us
    dot_general x6 -> x0, matrix products: 26.7 us -> none  [the longest x1 12.2 us: shards(): jnp.einsum('bhpn,bn->bhp', fresh_state, c_rows, precision=lax.Precision.H...]
    pallas_call x0 -> x6, Pallas kernels: none -> 13.2 us  [call(): pl.pallas_call(kernel, out_shape=out, in_specs=ins, out_specs=tuple(outs...]
    reduce_scatter x1 -> x0, waiting for transfers between devices: 12.6 us -> none  [shards(): lax.psum_scatter(branch_part, 'tp', scatter_dimension=1, tiled=True)]
    all_gather x2 -> x0, blocking collectives: 12.1 us -> none  [the longest x1 6.63 us: shards(): lax.all_gather(hidden, 'tp', axis=1, tiled=True).astype(jnp.float32)]
    select_n x6 -> x0, other arithmetic: 11.5 us -> none  [the longest x1 7.99 us: shards(): jnp.where(is_live[:, None, None, None], fresh_state, ssm_state)]
    ppermute x0 -> x9, starting transfers between devices: none -> 8.6 us  [spread_out(): lax.ppermute(v, 'tp', [(i, (i + k) % n) for i in range(n)])]
    psum x1 -> x0, blocking collectives: 7.27 us -> none  [shards(): sq_total = lax.psum(part_sq, 'tp')]
    unnamed x19 -> x10, local copies, waits for them, and re-layouts: 4.2 us -> 10.9 us
  transfers between devices with their start and end apart: 1 -> 9, of which waited for: 1 -> 0; matrix products, arithmetic and copies ran while one was open for 1% -> 10% of each run, Pallas kernels for 0% -> 25%
where the time goes in v1:
time: 37.8 us; the launch traced here: 37.4 us
  local copies, waits for them, and re-layouts  14.8 us (39%)
  Pallas kernels  13.2 us (35%)
  starting transfers between devices  8.6 us (23%)
  between operations  0.76 us (2%)
    pallas_call x6, Pallas kernels, call(): pl.pallas_call(kernel, out_shape=out, in_specs=ins, out_specs=tuple(outs...  13.2 us
    unnamed x10, local copies, waits for them, and re-layouts  10.9 us
    ppermute x9, starting transfers between devices, spread_out(): lax.ppermute(v, 'tp', [(i, (i + k) % n) for i in range(n)])  8.6 us
    reshape x3, local copies, waits for them, and re-layouts, shards(): row = lambda v: v.reshape(1, -1)  3.89 us
  transfers between devices with their start and end apart: 9, of which 0 were waited for; matrix products, arithmetic and copies ran while one was open for 10% of the time, Pallas kernels for 25%

profile of v1, /device:TPU:0, one launch (start us, length us, event | category | flops | bytes accessed | tf_op | source)
XLA Modules:
  0.0 37.4 jit_solution(3826244279926514972)
XLA Ops:
  0.6 3.0 %collective-permute-start.1 = (bf16[16,640]{1,0:T(8,128)(2,1)}, bf16[16,640]{1,0:T(8,128)(2,1)S(1)}, u32[]{:S(2)}, u32[]{:S(2)}) collective-permute-start(bf16[16,640]{1,0:T(8,128)(2,1)} %refs_0_.1), channel_id=1, source_target_pairs={{0,8},{4,12},{8,0},{12,4},{1,9},{5,13},{9,1},{13,5},{2,10},{6,14},... | collective-permute-start | bytes 61448 | tf_op jit(solution)/shard_map/ppermute | solution.py:239
  3.7 0.0 collective-permute-start
  3.7 1.7 %collective-permute-start.2 = (bf16[16,640]{1,0:T(8,128)(2,1)}, bf16[16,640]{1,0:T(8,128)(2,1)S(1)}, u32[]{:S(2)}, u32[]{:S(2)}) collective-permute-start(bf16[16,640]{1,0:T(8,128)(2,1)} %refs_0_.1), channel_id=1, source_target_pairs={{0,12},{4,0},{8,4},{12,8},{1,13},{5,1},{9,5},{13,9},{2,14},{6,2},{... | collective-permute-start | bytes 61448 | tf_op jit(solution)/shard_map/ppermute | solution.py:239
  5.4 1.3 %reshape.42.refs_11_ = bf16[1,1280]{1,0:T(2,128)(2,1)} reshape(bf16[1280]{0:T(1024)(128)(2,1)} %param.27) | data formatting | bytes 5120 | tf_op jit(solution)/shard_map/reshape | solution.py:249
  6.7 1.3 %reshape.39.refs_1_ = f32[1,1280]{1,0:T(1,128)} reshape(f32[1280]{0:T(1024)} %param.36) | data formatting | bytes 10240 | tf_op jit(solution)/shard_map/reshape | solution.py:249
  8.0 1.3 %reshape.38.refs_0_ = f32[1,2560]{1,0:T(1,128)} reshape(f32[2560]{0:T(1024)} %param.21) | data formatting | bytes 20480 | tf_op jit(solution)/shard_map/reshape | solution.py:249
  9.3 1.3 %prep.1 = (f32[1,2560]{1,0:T(1,128)S(1)}, f32[1,1280]{1,0:T(1,128)S(1)}, f32[16,16]{1,0:T(8,128)S(1)}, bf16[16,16]{1,0:T(8,128)(2,1)S(1)}, bf16[64,2560]{1,0:T(8...) custom-call(f32[1,2560]{1,0:T(1,128)} %reshape.38.refs_0_, ...), custom_call_target="tpu_custom_call" | custom-call | flops 4000000 | bytes 16000000 | tf_op jit(solution)/shard_map/prep/pallas_call | solution.py:226
  10.7 0.0 copy-start.4
  10.7 0.7 %copy-done.4 = bf16[16,640]{1,0:T(8,128)(2,1)S(1)} copy-done((bf16[16,640]{1,0:T(8,128)(2,1)S(1)}, bf16[16,640]{1,0:T(8,128)(2,1)}, u32[]{:S(2)}) %copy-start.4) | copy-done | bytes 20504
  11.4 0.3 bc.1
  11.7 0.1 collective-permute-start.5
  11.8 0.4 %collective-permute-start.4 = (bf16[16,64]{1,0:T(8,128)(2,1)S(1)}, bf16[16,64]{1,0:T(8,128)(2,1)S(1)}, u32[]{:S(2)}, u32[]{:S(2)}) collective-permute-start(bf16[16,64]{1,0:T(8,128)(2,1)S(1)} %get-tuple-element.45.refs_0_), channel_id=1, source_target_pairs={{0,8},{4,12},{8,0},{12,4},{1,9},{5,13},{9,1},{13,5},{2,10},{6,14},... | collective-permute-start | bytes 6152 | tf_op jit(solution)/shard_map/ppermute | solution.py:239
  12.2 0.1 collective-permute-start.3
  12.3 2.9 %copy-done.1 = bf16[2560,1280]{1,0:T(8,128)(2,1)S(1)} copy-done((bf16[2560,1280]{1,0:T(8,128)(2,1)S(1)}, bf16[2560,1280]{1,0:T(8,128)(2,1)}, u32[]{:S(2)}) %copy-start.1) | copy-done | bytes 6553624
  15.2 2.9 %copy-done.2 = bf16[2560,1280]{1,0:T(8,128)(2,1)S(1)} copy-done((bf16[2560,1280]{1,0:T(8,128)(2,1)S(1)}, bf16[2560,1280]{1,0:T(8,128)(2,1)}, u32[]{:S(2)}) %copy-start.2) | copy-done | bytes 6553624
  18.0 2.3 %proj.1 = (bf16[16,1280]{1,0:T(8,128)(2,1)S(1)}, f32[16,1280]{1,0:T(8,128)S(1)}, f32[16,1280]{1,0:T(8,128)S(1)}, f32[16,1280]{1,0:T(8,128)S(1)}, bf16[32,1280]{1...) custom-call(bf16[16,2560]{1,0:T(8,128)(2,1)S(1)} %get-tuple-element.46.normed_ref, bf16[2560,1280]{1,0:T(8,128)(2,1)S(1)} %copy-done.1, ...), custom_call_target="tpu_custom_call" | custom-call | flops 200000000 | bytes 14000000 | tf_op jit(solution)/shard_map/proj/pallas_call | solution.py:226
  20.4 1.6 %copy-done = f32[16,20,64,128]{3,2,1,0:T(8,128)S(1)} copy-done((f32[16,20,64,128]{3,2,1,0:T(8,128)S(1)}, f32[16,20,64,128]{3,2,1,0:T(8,128)}, u32[]{:S(2)}) %copy-start) | copy-done | bytes 10485784
  22.0 2.9 %copy-done.3 = bf16[1280,2560]{1,0:T(8,128)(2,1)S(1)} copy-done((bf16[1280,2560]{1,0:T(8,128)(2,1)S(1)}, bf16[1280,2560]{1,0:T(8,128)(2,1)}, u32[]{:S(2)}) %copy-start.3) | copy-done | bytes 6553624
  24.9 2.8 %out.1 = (bf16[16,768]{1,0:T(8,128)(2,1)S(1)}, bf16[16,768]{1,0:T(8,128)(2,1)S(1)}, bf16[16,768]{1,0:T(8,128)(2,1)S(1)}, f32[16,768]{1,0:T(8,128)S(1)}, bf16[16,256]{1,0:T(8,128)(2,1)S(1)}) custom-call(bf16[16,64]{1,0:T(8,128)(2,1)S(1)} %get-tuple-element.45.refs_0_, bf16[16,64]{1,0:T(8,128)(2,1)S(1)} %collective-permute-done.3.refs_1_, ...), custom_call_target="tpu_custom_call" | custom-call | flops 200000000 | bytes 14000000 | tf_op jit(solution)/shard_map/out/pallas_call | solution.py:226
  27.7 1.8 %collective-permute-start.6 = (bf16[16,768]{1,0:T(8,128)(2,1)S(1)}, bf16[16,768]{1,0:T(8,128)(2,1)S(1)}, u32[]{:S(2)}, u32[]{:S(2)}) collective-permute-start(bf16[16,768]{1,0:T(8,128)(2,1)S(1)} %get-tuple-element.58), channel_id=1, source_target_pairs={{0,4},{4,8},{8,12},{12,0},{1,5},{5,9},{9,13},{13,1},{2,6},{6,10},{... | collective-permute-start | bytes 73736 | tf_op jit(solution)/shard_map/ppermute | solution.py:239
  29.4 0.3 collective-permute-start.7
  29.8 1.2 %collective-permute-start.8 = (bf16[16,768]{1,0:T(8,128)(2,1)S(1)}, bf16[16,768]{1,0:T(8,128)(2,1)S(1)}, u32[]{:S(2)}, u32[]{:S(2)}) collective-permute-start(bf16[16,768]{1,0:T(8,128)(2,1)S(1)} %get-tuple-element.60), channel_id=1, source_target_pairs={{0,12},{4,0},{8,4},{12,8},{1,13},{5,1},{9,5},{13,9},{2,14},{6,2},{... | collective-permute-start | bytes 73736 | tf_op jit(solution)/shard_map/ppermute | solution.py:239
  31.0 5.6 %state.1 = (f32[16,1280,128]{2,1,0:T(8,128)}, bf16[3,16,1280]{2,1,0:T(8,128)(2,1)}, bf16[3,16,64]{2,1,0:T(8,128)(2,1)}) custom-call(f32[16,1280,128]{2,1,0:T(8,128)S(1)} %bitcast.14, bf16[32,1280]{1,0:T(8,128)(2,1)S(1)} %get-tuple-element.61.u_ref, f32[16,20,128]{2,1,0:T(8,128)S(1)} %get-tuple-element.62.dec_ref, ...), custom_call_target="tpu_custom_call" | custom-call | flops 200000000 | bytes 14000000 | tf_op jit(solution)/shard_map/state/pallas_call | solution.py:226
  36.6 0.8 %final.1 = bf16[16,640]{1,0:T(8,128)(2,1)} custom-call(bf16[16,640]{1,0:T(8,128)(2,1)S(1)} %get-tuple-element.38.hid_ref, f32[16,128]{1,0:T(8,128)S(1)} %get-tuple-element.39.live_ref, f32[16,768]{1,0:T(8,128)S(1)} %get-tuple-element.57.own_ref, bf16[16,768]{1,0:T(8,128)(2,1)S(1)} %collective-permute-done.6.refs_0_, ...), custom_call_target="tpu_custom_call" | custom-call | flops 1000000 | bytes 100000 | tf_op jit(solution)/shard_map/final/pallas_call | solution.py:226
  (13 shorter events, 0.0 us)
Async XLA Ops:
  0.6 10.0 %collective-permute-start.1 = (bf16[16,640]{1,0:T(8,128)(2,1)}, bf16[16,640]{1,0:T(8,128)(2,1)S(1)}, u32[]{:S(2)}, u32[]{:S(2)}) collective-permute-start(bf16[16,640]{1,0:T(8,128)(2,1)} %refs_0_.1), channel_id=1, source_target_pairs={{0,8},{4,12},{8,0},{12,4},{1,9},{5,13},{9,1},{13,5},{2,10},{6,14},... | collective-permute-start | bytes 61448 | tf_op jit(solution)/shard_map/ppermute | solution.py:239
  3.7 7.0 %collective-permute-start = (bf16[16,640]{1,0:T(8,128)(2,1)}, bf16[16,640]{1,0:T(8,128)(2,1)S(1)}, u32[]{:S(2)}, u32[]{:S(2)}) collective-permute-start(bf16[16,640]{1,0:T(8,128)(2,1)} %refs_0_.1), channel_id=1, source_target_pairs={{0,4},{4,8},{8,12},{12,0},{1,5},{5,9},{9,13},{13,1},{2,6},{6,10},{... | collective-permute-start | bytes 61448 | tf_op jit(solution)/shard_map/ppermute | solution.py:239
  3.7 7.0 %collective-permute-start.2 = (bf16[16,640]{1,0:T(8,128)(2,1)}, bf16[16,640]{1,0:T(8,128)(2,1)S(1)}, u32[]{:S(2)}, u32[]{:S(2)}) collective-permute-start(bf16[16,640]{1,0:T(8,128)(2,1)} %refs_0_.1), channel_id=1, source_target_pairs={{0,12},{4,0},{8,4},{12,8},{1,13},{5,1},{9,5},{13,9},{2,14},{6,2},{... | collective-permute-start | bytes 61448 | tf_op jit(solution)/shard_map/ppermute | solution.py:239
  10.7 0.7 %copy-start.4 = (bf16[16,640]{1,0:T(8,128)(2,1)S(1)}, bf16[16,640]{1,0:T(8,128)(2,1)}, u32[]{:S(2)}) copy-start(bf16[16,640]{1,0:T(8,128)(2,1)} %refs_0_.1) | copy-start | bytes 61444
  11.7 8.6 %collective-permute-start.5 = (bf16[16,64]{1,0:T(8,128)(2,1)S(1)}, bf16[16,64]{1,0:T(8,128)(2,1)S(1)}, u32[]{:S(2)}, u32[]{:S(2)}) collective-permute-start(bf16[16,64]{1,0:T(8,128)(2,1)S(1)} %get-tuple-element.45.refs_0_), channel_id=1, source_target_pairs={{0,12},{4,0},{8,4},{12,8},{1,13},{5,1},{9,5},{13,9},{2,14},{6,2},{... | collective-permute-start | bytes 6152 | tf_op jit(solution)/shard_map/ppermute | solution.py:239
  11.8 8.6 %collective-permute-start.4 = (bf16[16,64]{1,0:T(8,128)(2,1)S(1)}, bf16[16,64]{1,0:T(8,128)(2,1)S(1)}, u32[]{:S(2)}, u32[]{:S(2)}) collective-permute-start(bf16[16,64]{1,0:T(8,128)(2,1)S(1)} %get-tuple-element.45.refs_0_), channel_id=1, source_target_pairs={{0,8},{4,12},{8,0},{12,4},{1,9},{5,13},{9,1},{13,5},{2,10},{6,14},... | collective-permute-start | bytes 6152 | tf_op jit(solution)/shard_map/ppermute | solution.py:239
  12.2 8.2 %collective-permute-start.3 = (bf16[16,64]{1,0:T(8,128)(2,1)S(1)}, bf16[16,64]{1,0:T(8,128)(2,1)S(1)}, u32[]{:S(2)}, u32[]{:S(2)}) collective-permute-start(bf16[16,64]{1,0:T(8,128)(2,1)S(1)} %get-tuple-element.45.refs_0_), channel_id=1, source_target_pairs={{0,4},{4,8},{8,12},{12,0},{1,5},{5,9},{9,13},{13,1},{2,6},{6,10},{... | collective-permute-start | bytes 6152 | tf_op jit(solution)/shard_map/ppermute | solution.py:239
  12.3 2.9 %copy-start.1 = (bf16[2560,1280]{1,0:T(8,128)(2,1)S(1)}, bf16[2560,1280]{1,0:T(8,128)(2,1)}, u32[]{:S(2)}) copy-start(bf16[2560,1280]{1,0:T(8,128)(2,1)} %xw_ref.1) | copy-start | bytes 19660804
  15.2 2.9 %copy-start.2 = (bf16[2560,1280]{1,0:T(8,128)(2,1)S(1)}, bf16[2560,1280]{1,0:T(8,128)(2,1)}, u32[]{:S(2)}) copy-start(bf16[2560,1280]{1,0:T(8,128)(2,1)} %zw_ref.1) | copy-start | bytes 19660804
  18.0 4.0 %copy-start = (f32[16,20,64,128]{3,2,1,0:T(8,128)S(1)}, f32[16,20,64,128]{3,2,1,0:T(8,128)}, u32[]{:S(2)}) copy-start(f32[16,20,64,128]{3,2,1,0:T(8,128)} %param.35) | copy-start | bytes 31457284
  22.0 2.9 %copy-start.3 = (bf16[1280,2560]{1,0:T(8,128)(2,1)S(1)}, bf16[1280,2560]{1,0:T(8,128)(2,1)}, u32[]{:S(2)}) copy-start(bf16[1280,2560]{1,0:T(8,128)(2,1)} %refs_10_.3) | copy-start | bytes 19660804
  27.7 8.9 %collective-permute-start.6 = (bf16[16,768]{1,0:T(8,128)(2,1)S(1)}, bf16[16,768]{1,0:T(8,128)(2,1)S(1)}, u32[]{:S(2)}, u32[]{:S(2)}) collective-permute-start(bf16[16,768]{1,0:T(8,128)(2,1)S(1)} %get-tuple-element.58), channel_id=1, source_target_pairs={{0,4},{4,8},{8,12},{12,0},{1,5},{5,9},{9,13},{13,1},{2,6},{6,10},{... | collective-permute-start | bytes 73736 | tf_op jit(solution)/shard_map/ppermute | solution.py:239
  29.4 7.1 %collective-permute-start.7 = (bf16[16,768]{1,0:T(8,128)(2,1)S(1)}, bf16[16,768]{1,0:T(8,128)(2,1)S(1)}, u32[]{:S(2)}, u32[]{:S(2)}) collective-permute-start(bf16[16,768]{1,0:T(8,128)(2,1)S(1)} %get-tuple-element.59), channel_id=1, source_target_pairs={{0,8},{4,12},{8,0},{12,4},{1,9},{5,13},{9,1},{13,5},{2,10},{6,14},... | collective-permute-start | bytes 73736 | tf_op jit(solution)/shard_map/ppermute | solution.py:239
  29.8 6.8 %collective-permute-start.8 = (bf16[16,768]{1,0:T(8,128)(2,1)S(1)}, bf16[16,768]{1,0:T(8,128)(2,1)S(1)}, u32[]{:S(2)}, u32[]{:S(2)}) collective-permute-start(bf16[16,768]{1,0:T(8,128)(2,1)S(1)} %get-tuple-element.60), channel_id=1, source_target_pairs={{0,12},{4,0},{8,4},{12,8},{1,13},{5,1},{9,5},{13,9},{2,14},{6,2},{... | collective-permute-start | bytes 73736 | tf_op jit(solution)/shard_map/ppermute | solution.py:239

commit v2 on v1

--- a/solution.py
+++ b/solution.py
@@ -8,6 +8,8 @@
 
 F32 = jnp.float32
 BF16 = jnp.bfloat16
+DEPTH = 8
+LEAD = 2e10
 NT = (((1,), (1,)), ((), ()))
 TN = (((0,), (0,)), ((), ()))
 EPS = 1e-05
@@ -49,15 +51,21 @@
         next_ref[k] = jnp.where(live_slot, newer, st_ref[k].astype(F32)).astype(BF16)
 
 
+def load_kernel(src_ref, dst_ref, sem):
+    copy = pltpu.make_async_copy(src_ref, dst_ref, sem)
+    copy.start()
+    copy.wait()
+
+
 def prep_kernel(count, *refs):
     src, refs = refs[:count], refs[count:]
     (gain_ref, ngain_ref, own_ref, live_own_ref, bcw_ref, dtw_ref, bcst_ref, bcbase_ref, bctap_ref, xst_ref,
-     xbase_ref, xtap_ref, dtb_ref, rate_ref, skip_ref, hid_ref, live_ref) = refs[:17]
-    slot_s, act_s, bccw_s, bccb_s, xcw_s, xcb_s, sems = refs[17:]
-    dst = (gain_ref, ngain_ref, slot_s, act_s, bcw_ref, dtw_ref, bcst_ref, bccw_s, bccb_s, xst_ref, xcw_s, xcb_s,
-           dtb_ref, rate_ref, skip_ref, hid_ref)
+     xbase_ref, xtap_ref, dtb_ref, rate_ref, skip_ref, live_ref) = refs[:16]
+    gain_s, ngain_s, slot_s, act_s, bccw_s, bccb_s, xcw_s, xcb_s, sems = refs[16:]
+    dst = (gain_s, ngain_s, slot_s, act_s, bcw_ref, dtw_ref, bcst_ref, bccw_s, bccb_s, xst_ref, xcw_s, xcb_s,
+           dtb_ref, rate_ref, skip_ref)
     copies = [pltpu.make_async_copy(a, b, sems.at[i]) for i, (a, b) in enumerate(zip(src, dst))]
-    order = (2, 3, 6, 7, 8, 9, 10, 11, 4, 5, 0, 1, 12, 13, 14, 15)
+    order = (2, 3, 6, 7, 8, 9, 10, 11, 0, 1, 4, 5, 12, 13, 14)
     for i in order:
         copies[i].start()
     copies[2].wait()
@@ -73,18 +81,22 @@
         for i in waits:
             copies[i].wait()
         weight = cw[...].astype(F32)
-        acc = jnp.broadcast_to(cb[...].astype(F32), base.shape)
+        acc = jnp.broadcast_to(cb[...].astype(F32).reshape(1, -1), base.shape)
         for k in range(3):
             acc = acc + jnp.dot(own_b, st[k], preferred_element_type=F32) * weight[k:k + 1]
         base[...] = acc
         tap[...] = weight[3:4]
-    for i in (4, 5, 0, 1, 12, 13, 14, 15):
+    for i in (0, 1):
+        copies[i].wait()
+    gain_ref[...] = gain_s[...].reshape(1, -1)
+    ngain_ref[...] = ngain_s[...].reshape(1, -1)
+    for i in (4, 5, 12, 13, 14):
         copies[i].wait()
 
 
 def bc_kernel(n, *refs):
     parts, refs = refs[:n], refs[n:]
-    gain_ref, own_ref, w_ref, base_ref, tap_ref, normed_ref, bc_ref, proj_ref = refs
+    gain_ref, _, w_ref, base_ref, tap_ref, normed_ref, bc_ref, proj_ref = refs
     me = lax.axis_index("tp")
     blocks = [p[...] for p in parts]
     width = blocks[0].shape[1]
@@ -103,7 +115,9 @@
 
 
 def in_kernel(hp, normed_ref, xw_ref, zw_ref, dtw_ref, base_ref, tap_ref, dtb_ref, rate_ref, skip_ref, own_ref,
-              live_ref, xproj_ref, g1_ref, g2_ref, g3_ref, u_ref, dec_ref):
+              live_ref, ow_ref, xproj_ref, g1_ref, g2_ref, g3_ref, u_ref, dec_ref, owv_ref, sem):
+    fetch = pltpu.make_async_copy(ow_ref, owv_ref, sem)
+    fetch.start()
     normed = normed_ref[...]
     seqs = normed.shape[0]
     chans = xw_ref.shape[1]
@@ -132,8 +146,12 @@
     g3_ref[...] = gate * (skip_w * x)
     u = jnp.where(live, u, 0.0)
     high = u.astype(BF16)
-    u_ref[:seqs] = high
-    u_ref[seqs:] = (u - high.astype(F32)).astype(BF16)
+    low = (u - high.astype(F32)).astype(BF16)
+    own_b = own_ref[...].astype(BF16)
+    u_slot = (lax.dot_general(own_b, high, TN, preferred_element_type=F32)
+              + lax.dot_general(own_b, low, TN, preferred_element_type=F32))
+    u_ref[...] = u_slot.T
+    fetch.wait()
 
 
 def out_kernel(n, *refs):
@@ -175,34 +193,36 @@
 
 
 def state_kernel(state_ref, u_ref, dec_ref, bcf_ref, own_ref, live_own_ref, xst_ref, xproj_ref, bcst_ref, bcproj_ref,
-                 next_ref, xnext_ref, bcnext_ref, ring, sems):
+                 next_ref, xnext_ref, bcnext_ref, ring, xkeep, bckeep, sems, pool_sems):
     seqs, chans, ns = state_ref.shape
     heads = dec_ref.shape[1]
     hp = chans // heads
-    own = own_ref[...] > 0.5
-    b_rows = bcf_ref[:, :ns].astype(F32)
-    u_rows = u_ref[...]
+    b_slot = lax.dot_general(own_ref[...].astype(BF16), bcf_ref[:, :ns], TN, preferred_element_type=F32)
     depth = ring.shape[0]
 
     def copy(s):
-        return pltpu.make_async_copy(ring.at[s // 2 % depth], next_ref.at[pl.ds(s, 2)], sems.at[s // 2 % depth])
-
-    for s in range(0, seqs, 2):
-        pair = jnp.concatenate([jnp.where(own[:, t:t + 1], b_rows, 0.0).astype(BF16) for t in (s, s + 1)], axis=1)
-        fresh = lax.dot_general(u_rows, jnp.concatenate([pair, pair], axis=0), TN, preferred_element_type=F32)
-        if s // 2 >= depth:
-            copy(s - 2 * depth).wait()
-        for t in range(2):
-            for h in range(heads):
-                rows = slice(h * hp, (h + 1) * hp)
-                ring[s // 2 % depth, t, rows, :] = (
-                    state_ref[s + t, rows, :] * dec_ref[s + t, h:h + 1, :] + fresh[rows, t * ns:(t + 1) * ns]
-                )
+        return pltpu.make_async_copy(ring.at[s % depth], next_ref.at[s], sems.at[s % depth])
+
+    for s in range(seqs):
+        if s >= depth:
+            copy(s - depth).wait()
+        for h in range(heads):
+            rows = slice(h * hp, (h + 1) * hp)
+            ring[s % depth, rows, :] = (
+                state_ref[s, rows, :] * dec_ref[s, h:h + 1, :] + u_ref[rows, s:s + 1] * b_slot[s:s + 1]
+            )
         copy(s).start()
-    shift_state(xst_ref, xproj_ref[...], live_own_ref[...], xnext_ref)
-    shift_state(bcst_ref, bcproj_ref[...], live_own_ref[...], bcnext_ref)
-    for s in range(max(0, seqs - 2 * depth), seqs, 2):
+        if s == seqs // 4:
+            shift_state(xst_ref, xproj_ref[...], live_own_ref[...], xkeep)
+            shift_state(bcst_ref, bcproj_ref[...], live_own_ref[...], bckeep)
+            pools = [pltpu.make_async_copy(xkeep, xnext_ref, pool_sems.at[0]),
+                     pltpu.make_async_copy(bckeep, bcnext_ref, pool_sems.at[1])]
+            for pool in pools:
+                pool.start()
+    for s in range(max(0, seqs - depth), seqs):
         copy(s).wait()
+    for pool in pools:
+        pool.wait()
 
 
 def final_kernel(chans, hid_ref, live_ref, own_ref, *refs):
@@ -247,40 +267,46 @@
     width = hidden.shape[1]
     bcw = bc_weight.shape[1]
     row = lambda v: v.reshape(1, -1)
+    pinned = lambda v: pltpu.with_memory_space_constraint(v, pltpu.HBM)
     sds = jax.ShapeDtypeStruct
     like = lambda v: sds(v.shape, v.dtype)
     state = ssm_state.reshape(seqs, chans, ns)
-    parts = [hidden] + spread_out([hidden] * (n - 1), n)
-    src = tuple(pltpu.with_memory_space_constraint(v, pltpu.HBM) for v in (row(in_gain), row(norm_gain), pool_slot.reshape(1, -1), row(active), bc_weight.T, dt_weight.T,
-           conv_bc_state.transpose(1, 0, 2), conv_bc_weight, row(conv_bc_bias), conv_x_state.transpose(1, 0, 2),
-           conv_x_weight, row(conv_x_bias), row(dt_bias), row(log_rate), row(skip_gain), hidden))
-    held = {i: pltpu.VMEM(src[i].shape, src[i].dtype) for i in (2, 3, 7, 8, 10, 11)}
-    (gain, ngain, own, live_own, bcw_v, dtw_v, bcst, bcbase, bctap, xst, xbase, xtap, dtb, rate, skip, hid, live) = call(
+    hid, = call(load_kernel, "load", (like(hidden),), [HB], (pinned(hidden),), scratch=[pltpu.SemaphoreType.DMA],
+                flops=LEAD, moved=1e5)
+    parts = [hid] + spread_out([hid] * (n - 1), n)
+    src = (in_gain, norm_gain, row(pool_slot), row(active), bc_weight.T, dt_weight.T, conv_bc_state.transpose(1, 0, 2),
+           conv_bc_weight, row(conv_bc_bias), conv_x_state.transpose(1, 0, 2), conv_x_weight, conv_x_bias, row(dt_bias),
+           row(log_rate), row(skip_gain))
+    held = {i: pltpu.VMEM(src[i].shape, src[i].dtype) for i in (0, 1, 2, 3, 7, 8, 10, 11)}
+    (gain, ngain, own, live_own, bcw_v, dtw_v, bcst, bcbase, bctap, xst, xbase, xtap, dtb, rate, skip, live) = call(
         functools.partial(prep_kernel, len(src)), "prep",
-        (like(src[0]), like(src[1]), sds((seqs, seqs), F32), sds((seqs, seqs), BF16), like(src[4]), like(src[5]),
+        (like(row(in_gain)), like(row(norm_gain)), sds((seqs, seqs), F32), sds((seqs, seqs), BF16), like(src[4]), like(src[5]),
          like(src[6]), sds((seqs, bcw), F32), sds((1, bcw), F32), like(src[9]), sds((seqs, chans), F32),
-         sds((1, chans), F32), like(src[12]), like(src[13]), like(src[14]), like(hidden), sds((seqs, 128), F32)),
-        [HB] * len(src), src, scratch=[*held.values(), pltpu.SemaphoreType.DMA((len(src),))], flops=4e6, moved=16e6)
+         sds((1, chans), F32), like(src[12]), like(src[13]), like(src[14]), sds((seqs, 128), F32)),
+        [HB] * len(src), tuple(map(pinned, src)), scratch=[*held.values(), pltpu.SemaphoreType.DMA((len(src),))], flops=4e6, moved=1e6)
     normed, bc_own, bcproj = call(
         functools.partial(bc_kernel, n), "bc",
         (sds((seqs, n * width), BF16), sds((seqs, bcw), BF16), sds((seqs, bcw), BF16)),
-        [VM] * (n + 5), (*parts, gain, own, bcw_v, bcbase, bctap), flops=4e6)
+        [VM] * (n + 5), (*parts, gain, state, bcw_v, bcbase, bctap), flops=4e6)
     bc_parts = [bc_own] + spread_out([bc_own] * (n - 1), n)
     wide = sds((seqs, chans), F32)
-    xproj, g1, g2, g3, u, dec = call(
+    xproj, g1, g2, g3, u, dec, out_w = call(
         functools.partial(in_kernel, hp), "proj",
-        (sds((seqs, chans), BF16), wide, wide, wide, sds((2 * seqs, chans), BF16), sds((seqs, heads, 128), F32)),
-        [VM] * 11, (normed, x_weight, z_weight, dtw_v, xbase, xtap, dtb, rate, skip, own, live), flops=2e8, moved=14e6)
+        (sds((seqs, chans), BF16), wide, wide, wide, sds((chans, seqs), F32), sds((seqs, heads, 128), F32),
+         like(out_weight)),
+        [VM] * 11 + [HB], (normed, x_weight, z_weight, dtw_v, xbase, xtap, dtb, rate, skip, own, live, pinned(out_weight)),
+        scratch=[pltpu.SemaphoreType.DMA], flops=1e6, moved=1e5)
     *sends, own_sum, bcf = call(
         functools.partial(out_kernel, n), "out",
         (*[sds((seqs, width + 128), BF16)] * (n - 1), sds((seqs, width + 128), F32), sds((seqs, n * bcw), BF16)),
-        [VM] * (n + 7), (*bc_parts, state, own, g1, g2, g3, ngain, out_weight),
+        [VM] * (n + 7), (*bc_parts, state, own, g1, g2, g3, ngain, out_w),
         scratch=[pltpu.VMEM((n, seqs, width + 128), F32)], flops=2e8, moved=14e6, mib=12)
     got = spread_out(sends, n)
     fresh, x_next, bc_next = call(
         state_kernel, "state", (like(state), like(xst), like(bcst)), [VM] * 10,
-        (state, u, dec, bcf, own, live_own, xst, xproj, bcst, bcproj), outs=(HB, VM, VM),
-        scratch=[pltpu.VMEM((4, 2, chans, ns), F32), pltpu.SemaphoreType.DMA((4,))], flops=2e8, moved=14e6, mib=12)
+        (state, u, dec, bcf, own, live_own, xst, xproj, bcst, bcproj), outs=(HB, HB, HB),
+        scratch=[pltpu.VMEM((DEPTH, chans, ns), F32), pltpu.VMEM(xst.shape, BF16), pltpu.VMEM(bcst.shape, BF16),
+                 pltpu.SemaphoreType.DMA((DEPTH,)), pltpu.SemaphoreType.DMA((2,))], flops=2e8, moved=14e6, mib=12)
     layer_out, = call(functools.partial(final_kernel, chans * n), "final", (like(hidden),), [VM] * (n + 2),
                       (hid, live, own_sum, *got))
     return (layer_out, x_next.transpose(1, 0, 2), bc_next.transpose(1, 0, 2), fresh.reshape(ssm_state.shape))

time: 37.8 us -> 24.6 us (0.65)
  local copies, waits for them, and re-layouts: 14.8 us -> 0.01 us
  waiting for transfers between devices: 0.02 us -> 1.24 us
  Pallas kernels: 13.2 us -> 14.3 us
  starting transfers between devices: 8.6 us -> 8.16 us
    unnamed x10 -> x6, local copies, waits for them, and re-layouts: 10.9 us -> 0.01 us
    reshape x3 -> x0, local copies, waits for them, and re-layouts: 3.89 us -> none  [shards(): row = lambda v: v.reshape(1, -1)]
    ppermute x9, waiting for transfers between devices: 0.02 us -> 1.24 us  [spread_out(): lax.ppermute(v, 'tp', [(i, (i + k) % n) for i in range(n)])]
    pallas_call x6 -> x7, Pallas kernels: 13.2 us -> 14.3 us  [call(): pl.pallas_call(kernel, out_shape=out, in_specs=ins, out_specs=tuple(outs...]
    ppermute x9, starting transfers between devices: 8.6 us -> 8.16 us  [spread_out(): lax.ppermute(v, 'tp', [(i, (i + k) % n) for i in range(n)])]
  transfers between devices with their start and end apart: 9 -> 9, of which waited for: 0 -> 3; matrix products, arithmetic and copies ran while one was open for 10% -> 0% of each run, Pallas kernels for 25% -> 39%
where the time goes in v2:
time: 24.6 us; the launch traced here: 24.4 us
  Pallas kernels  14.3 us (58%)
  starting transfers between devices  8.16 us (33%)
  waiting for transfers between devices  1.24 us (5%)
  between operations  0.76 us (3%)
    pallas_call x7, Pallas kernels, call(): pl.pallas_call(kernel, out_shape=out, in_specs=ins, out_specs=tuple(outs...  14.3 us
    ppermute x9, starting transfers between devices, spread_out(): lax.ppermute(v, 'tp', [(i, (i + k) % n) for i in range(n)])  8.16 us
    ppermute x9, waiting for transfers between devices, spread_out(): lax.ppermute(v, 'tp', [(i, (i + k) % n) for i in range(n)])  1.24 us
  transfers between devices with their start and end apart: 9, of which 3 were waited for; matrix products, arithmetic and copies ran while one was open for 0% of the time, Pallas kernels for 39%

profile of v2, /device:TPU:0, one launch (start us, length us, event | category | flops | bytes accessed | tf_op | source)
XLA Modules:
  0.0 24.4 jit_solution(4782609032233441281)
XLA Ops:
  0.7 0.9 %load.1.refs_0_.hid_ref = bf16[16,640]{1,0:T(8,128)(2,1)S(1)} custom-call(bf16[16,640]{1,0:T(8,128)(2,1)} %src_ref.1), custom_call_target="tpu_custom_call" | custom-call | flops 20000000000 | bytes 100000 | tf_op jit(solution)/shard_map/load/pallas_call | solution.py:246
  1.5 0.0 copy-start.1
  1.6 2.5 %collective-permute-start.2 = (bf16[16,640]{1,0:T(8,128)(2,1)S(1)}, bf16[16,640]{1,0:T(8,128)(2,1)S(1)}, u32[]{:S(2)}, u32[]{:S(2)}) collective-permute-start(bf16[16,640]{1,0:T(8,128)(2,1)S(1)} %load.1.refs_0_.hid_ref), channel_id=1, source_target_pairs={{0,12},{4,0},{8,4},{12,8},{1,13},{5,1},{9,5},{13,9},{2,14},{6,2},{... | collective-permute-start | bytes 61448 | tf_op jit(solution)/shard_map/ppermute | solution.py:259
  4.0 0.6 %collective-permute-start.1 = (bf16[16,640]{1,0:T(8,128)(2,1)S(1)}, bf16[16,640]{1,0:T(8,128)(2,1)S(1)}, u32[]{:S(2)}, u32[]{:S(2)}) collective-permute-start(bf16[16,640]{1,0:T(8,128)(2,1)S(1)} %load.1.refs_0_.hid_ref), channel_id=1, source_target_pairs={{0,8},{4,12},{8,0},{12,4},{1,9},{5,13},{9,1},{13,5},{2,10},{6,14},... | collective-permute-start | bytes 61448 | tf_op jit(solution)/shard_map/ppermute | solution.py:259
  4.7 0.2 collective-permute-start
  4.8 2.1 %prep.1 = (f32[1,2560]{1,0:T(1,128)S(1)}, f32[1,1280]{1,0:T(1,128)S(1)}, f32[16,16]{1,0:T(8,128)S(1)}, bf16[16,16]{1,0:T(8,128)(2,1)S(1)}, bf16[64,2560]{1,0:T(8...) custom-call(f32[2560]{0:T(1024)} %refs_0_.1, ...), custom_call_target="tpu_custom_call" | custom-call | flops 4000000 | bytes 1000000 | tf_op jit(solution)/shard_map/prep/pallas_call | solution.py:246
  6.9 0.0 collective-permute-done.2.refs_3_
  6.9 1.0 %collective-permute-done.1.refs_2_ = bf16[16,640]{1,0:T(8,128)(2,1)S(1)} collective-permute-done((bf16[16,640]{1,0:T(8,128)(2,1)S(1)}, bf16[16,640]{1,0:T(8,128)(2,1)S(1)}, u32[]{:S(2)}, u32[]{:S(2)}) %collective-permute-start.1) | collective-permute-done | bytes 20512 | tf_op jit(solution)/shard_map/ppermute | solution.py:259
  8.0 0.1 collective-permute-done.refs_1_
  8.0 0.3 %bc.1 = (bf16[16,2560]{1,0:T(8,128)(2,1)S(1)}, bf16[16,64]{1,0:T(8,128)(2,1)S(1)}, bf16[16,64]{1,0:T(8,128)(2,1)S(1)}) custom-call(bf16[16,640]{1,0:T(8,128)(2,1)S(1)} %load.1.refs_0_.hid_ref, bf16[16,640]{1,0:T(8,128)(2,1)S(1)} %collective-permute-done.refs_1_, bf16[16,640]{1,0:T(8,128)(2,1)S(1)} %collective-permute-done.1.refs_2_, ...), custom_call_target="tpu_custom_call" | custom-call | flops 4000000 | bytes 100000 | tf_op jit(solution)/shard_map/bc/pallas_call | solution.py:246
  8.4 0.6 %collective-permute-start.5 = (bf16[16,64]{1,0:T(8,128)(2,1)S(1)}, bf16[16,64]{1,0:T(8,128)(2,1)S(1)}, u32[]{:S(2)}, u32[]{:S(2)}) collective-permute-start(bf16[16,64]{1,0:T(8,128)(2,1)S(1)} %get-tuple-element.43.refs_0_), channel_id=1, source_target_pairs={{0,12},{4,0},{8,4},{12,8},{1,13},{5,1},{9,5},{13,9},{2,14},{6,2},{... | collective-permute-start | bytes 6152 | tf_op jit(solution)/shard_map/ppermute | solution.py:259
  8.9 1.4 %collective-permute-start.4 = (bf16[16,64]{1,0:T(8,128)(2,1)S(1)}, bf16[16,64]{1,0:T(8,128)(2,1)S(1)}, u32[]{:S(2)}, u32[]{:S(2)}) collective-permute-start(bf16[16,64]{1,0:T(8,128)(2,1)S(1)} %get-tuple-element.43.refs_0_), channel_id=1, source_target_pairs={{0,8},{4,12},{8,0},{12,4},{1,9},{5,13},{9,1},{13,5},{2,10},{6,14},... | collective-permute-start | bytes 6152 | tf_op jit(solution)/shard_map/ppermute | solution.py:259
  10.3 0.0 collective-permute-start.3
  10.3 2.9 %proj.1 = (bf16[16,1280]{1,0:T(8,128)(2,1)S(1)}, f32[16,1280]{1,0:T(8,128)S(1)}, f32[16,1280]{1,0:T(8,128)S(1)}, f32[16,1280]{1,0:T(8,128)S(1)}, f32[1280,16]{1,...) custom-call(bf16[16,2560]{1,0:T(8,128)(2,1)S(1)} %get-tuple-element.45.normed_ref, ...), custom_call_target="tpu_custom_call" | custom-call | flops 1000000 | bytes 100000 | tf_op jit(solution)/shard_map/proj/pallas_call | solution.py:246
  13.2 0.0 collective-permute-done.5.refs_3_
  13.2 0.0 collective-permute-done.4.refs_2_
  13.2 0.1 collective-permute-done.3.refs_1_
  13.3 2.8 %out.1 = (bf16[16,768]{1,0:T(8,128)(2,1)S(1)}, bf16[16,768]{1,0:T(8,128)(2,1)S(1)}, bf16[16,768]{1,0:T(8,128)(2,1)S(1)}, f32[16,768]{1,0:T(8,128)S(1)}, bf16[16,256]{1,0:T(8,128)(2,1)S(1)}) custom-call(bf16[16,64]{1,0:T(8,128)(2,1)S(1)} %get-tuple-element.43.refs_0_, bf16[16,64]{1,0:T(8,128)(2,1)S(1)} %collective-permute-done.3.refs_1_, ...), custom_call_target="tpu_custom_call" | custom-call | flops 200000000 | bytes 14000000 | tf_op jit(solution)/shard_map/out/pallas_call | solution.py:246
  16.2 0.7 %collective-permute-start.6 = (bf16[16,768]{1,0:T(8,128)(2,1)S(1)}, bf16[16,768]{1,0:T(8,128)(2,1)S(1)}, u32[]{:S(2)}, u32[]{:S(2)}) collective-permute-start(bf16[16,768]{1,0:T(8,128)(2,1)S(1)} %get-tuple-element.58), channel_id=1, source_target_pairs={{0,4},{4,8},{8,12},{12,0},{1,5},{5,9},{9,13},{13,1},{2,6},{6,10},{... | collective-permute-start | bytes 73736 | tf_op jit(solution)/shard_map/ppermute | solution.py:259
  16.9 1.4 %collective-permute-start.7 = (bf16[16,768]{1,0:T(8,128)(2,1)S(1)}, bf16[16,768]{1,0:T(8,128)(2,1)S(1)}, u32[]{:S(2)}, u32[]{:S(2)}) collective-permute-start(bf16[16,768]{1,0:T(8,128)(2,1)S(1)} %get-tuple-element.59), channel_id=1, source_target_pairs={{0,8},{4,12},{8,0},{12,4},{1,9},{5,13},{9,1},{13,5},{2,10},{6,14},... | collective-permute-start | bytes 73736 | tf_op jit(solution)/shard_map/ppermute | solution.py:259
  18.2 0.9 %collective-permute-start.8 = (bf16[16,768]{1,0:T(8,128)(2,1)S(1)}, bf16[16,768]{1,0:T(8,128)(2,1)S(1)}, u32[]{:S(2)}, u32[]{:S(2)}) collective-permute-start(bf16[16,768]{1,0:T(8,128)(2,1)S(1)} %get-tuple-element.60), channel_id=1, source_target_pairs={{0,12},{4,0},{8,4},{12,8},{1,13},{5,1},{9,5},{13,9},{2,14},{6,2},{... | collective-permute-start | bytes 73736 | tf_op jit(solution)/shard_map/ppermute | solution.py:259
  19.1 4.5 %state.1 = (f32[16,1280,128]{2,1,0:T(8,128)}, bf16[3,16,1280]{2,1,0:T(8,128)(2,1)}, bf16[3,16,64]{2,1,0:T(8,128)(2,1)}) custom-call(f32[16,1280,128]{2,1,0:T(8,128)S(1)} %bitcast.15, f32[1280,16]{1,0:T(8,128)S(1)} %get-tuple-element.61.u_ref, f32[16,20,128]{2,1,0:T(8,128)S(1)} %get-tuple-element.62.dec_ref, bf16[16,256]{1,0:T(8,128)(2,1)S(1)} %get-tuple-element.63.bcf_ref, ...), custom_call_target="tpu_custom_call" | custom-call | flops 200000000 | bytes 14000000 | tf_op jit(solution)/shard_map/state/pallas_call | solution.py:246
  23.6 0.0 collective-permute-done.6.refs_0_
  23.7 0.8 %final.1 = bf16[16,640]{1,0:T(8,128)(2,1)} custom-call(bf16[16,640]{1,0:T(8,128)(2,1)S(1)} %load.1.refs_0_.hid_ref, f32[16,128]{1,0:T(8,128)S(1)} %get-tuple-element.38.live_ref, f32[16,768]{1,0:T(8,128)S(1)} %get-tuple-element.57.own_ref, bf16[16,768]{1,0:T(8,128)(2,1)S(1)} %collective-permute-done.6.refs_0_, ...), custom_call_target="tpu_custom_call" | custom-call | flops 1000000 | bytes 100000 | tf_op jit(solution)/shard_map/final/pallas_call | solution.py:246
  (7 shorter events, 0.0 us)
Async XLA Ops:
  0.6 7.4 %copy-start = (f32[16,20,64,128]{3,2,1,0:T(8,128)S(1)}, f32[16,20,64,128]{3,2,1,0:T(8,128)}, u32[]{:S(2)}) copy-start(f32[16,20,64,128]{3,2,1,0:T(8,128)} %param.35) | copy-start | bytes 31457284
  0.6 9.7 %copy-start.2 = (bf16[2560,1280]{1,0:T(8,128)(2,1)S(1)}, bf16[2560,1280]{1,0:T(8,128)(2,1)}, u32[]{:S(2)}) copy-start(bf16[2560,1280]{1,0:T(8,128)(2,1)} %zw_ref.1) | copy-start | bytes 19660804
  1.5 8.7 %copy-start.1 = (bf16[2560,1280]{1,0:T(8,128)(2,1)S(1)}, bf16[2560,1280]{1,0:T(8,128)(2,1)}, u32[]{:S(2)}) copy-start(bf16[2560,1280]{1,0:T(8,128)(2,1)} %xw_ref.1) | copy-start | bytes 19660804
  1.6 5.3 %collective-permute-start.2 = (bf16[16,640]{1,0:T(8,128)(2,1)S(1)}, bf16[16,640]{1,0:T(8,128)(2,1)S(1)}, u32[]{:S(2)}, u32[]{:S(2)}) collective-permute-start(bf16[16,640]{1,0:T(8,128)(2,1)S(1)} %load.1.refs_0_.hid_ref), channel_id=1, source_target_pairs={{0,12},{4,0},{8,4},{12,8},{1,13},{5,1},{9,5},{13,9},{2,14},{6,2},{... | collective-permute-start | bytes 61448 | tf_op jit(solution)/shard_map/ppermute | solution.py:259
  4.0 3.9 %collective-permute-start.1 = (bf16[16,640]{1,0:T(8,128)(2,1)S(1)}, bf16[16,640]{1,0:T(8,128)(2,1)S(1)}, u32[]{:S(2)}, u32[]{:S(2)}) collective-permute-start(bf16[16,640]{1,0:T(8,128)(2,1)S(1)} %load.1.refs_0_.hid_ref), channel_id=1, source_target_pairs={{0,8},{4,12},{8,0},{12,4},{1,9},{5,13},{9,1},{13,5},{2,10},{6,14},... | collective-permute-start | bytes 61448 | tf_op jit(solution)/shard_map/ppermute | solution.py:259
  4.7 3.4 %collective-permute-start = (bf16[16,640]{1,0:T(8,128)(2,1)S(1)}, bf16[16,640]{1,0:T(8,128)(2,1)S(1)}, u32[]{:S(2)}, u32[]{:S(2)}) collective-permute-start(bf16[16,640]{1,0:T(8,128)(2,1)S(1)} %load.1.refs_0_.hid_ref), channel_id=1, source_target_pairs={{0,4},{4,8},{8,12},{12,0},{1,5},{5,9},{9,13},{13,1},{2,6},{6,10},{... | collective-permute-start | bytes 61448 | tf_op jit(solution)/shard_map/ppermute | solution.py:259
  8.4 4.8 %collective-permute-start.5 = (bf16[16,64]{1,0:T(8,128)(2,1)S(1)}, bf16[16,64]{1,0:T(8,128)(2,1)S(1)}, u32[]{:S(2)}, u32[]{:S(2)}) collective-permute-start(bf16[16,64]{1,0:T(8,128)(2,1)S(1)} %get-tuple-element.43.refs_0_), channel_id=1, source_target_pairs={{0,12},{4,0},{8,4},{12,8},{1,13},{5,1},{9,5},{13,9},{2,14},{6,2},{... | collective-permute-start | bytes 6152 | tf_op jit(solution)/shard_map/ppermute | solution.py:259
  8.9 4.3 %collective-permute-start.4 = (bf16[16,64]{1,0:T(8,128)(2,1)S(1)}, bf16[16,64]{1,0:T(8,128)(2,1)S(1)}, u32[]{:S(2)}, u32[]{:S(2)}) collective-permute-start(bf16[16,64]{1,0:T(8,128)(2,1)S(1)} %get-tuple-element.43.refs_0_), channel_id=1, source_target_pairs={{0,8},{4,12},{8,0},{12,4},{1,9},{5,13},{9,1},{13,5},{2,10},{6,14},... | collective-permute-start | bytes 6152 | tf_op jit(solution)/shard_map/ppermute | solution.py:259
  10.3 3.0 %collective-permute-start.3 = (bf16[16,64]{1,0:T(8,128)(2,1)S(1)}, bf16[16,64]{1,0:T(8,128)(2,1)S(1)}, u32[]{:S(2)}, u32[]{:S(2)}) collective-permute-start(bf16[16,64]{1,0:T(8,128)(2,1)S(1)} %get-tuple-element.43.refs_0_), channel_id=1, source_target_pairs={{0,4},{4,8},{8,12},{12,0},{1,5},{5,9},{9,13},{13,1},{2,6},{6,10},{... | collective-permute-start | bytes 6152 | tf_op jit(solution)/shard_map/ppermute | solution.py:259
  16.2 7.5 %collective-permute-start.6 = (bf16[16,768]{1,0:T(8,128)(2,1)S(1)}, bf16[16,768]{1,0:T(8,128)(2,1)S(1)}, u32[]{:S(2)}, u32[]{:S(2)}) collective-permute-start(bf16[16,768]{1,0:T(8,128)(2,1)S(1)} %get-tuple-element.58), channel_id=1, source_target_pairs={{0,4},{4,8},{8,12},{12,0},{1,5},{5,9},{9,13},{13,1},{2,6},{6,10},{... | collective-permute-start | bytes 73736 | tf_op jit(solution)/shard_map/ppermute | solution.py:259
  16.9 6.8 %collective-permute-start.7 = (bf16[16,768]{1,0:T(8,128)(2,1)S(1)}, bf16[16,768]{1,0:T(8,128)(2,1)S(1)}, u32[]{:S(2)}, u32[]{:S(2)}) collective-permute-start(bf16[16,768]{1,0:T(8,128)(2,1)S(1)} %get-tuple-element.59), channel_id=1, source_target_pairs={{0,8},{4,12},{8,0},{12,4},{1,9},{5,13},{9,1},{13,5},{2,10},{6,14},... | collective-permute-start | bytes 73736 | tf_op jit(solution)/shard_map/ppermute | solution.py:259
  18.2 5.4 %collective-permute-start.8 = (bf16[16,768]{1,0:T(8,128)(2,1)S(1)}, bf16[16,768]{1,0:T(8,128)(2,1)S(1)}, u32[]{:S(2)}, u32[]{:S(2)}) collective-permute-start(bf16[16,768]{1,0:T(8,128)(2,1)S(1)} %get-tuple-element.60), channel_id=1, source_target_pairs={{0,12},{4,0},{8,4},{12,8},{1,13},{5,1},{9,5},{13,9},{2,14},{6,2},{... | collective-permute-start | bytes 73736 | tf_op jit(solution)/shard_map/ppermute | solution.py:259

commit v3 on v2

--- a/solution.py
+++ b/solution.py
@@ -8,7 +8,6 @@
 
 F32 = jnp.float32
 BF16 = jnp.bfloat16
-DEPTH = 8
 LEAD = 2e10
 NT = (((1,), (1,)), ((), ()))
 TN = (((0,), (0,)), ((), ()))
@@ -96,68 +95,88 @@
 
 def bc_kernel(n, *refs):
     parts, refs = refs[:n], refs[n:]
-    gain_ref, _, w_ref, base_ref, tap_ref, normed_ref, bc_ref, proj_ref = refs
+    gain_ref, bcw_ref, dtw_ref, base_ref, tap_ref, normed_ref, bc_ref, proj_ref, dt_ref = refs
+    bcw, heads = bc_ref.shape[1], dt_ref.shape[1]
     me = lax.axis_index("tp")
     blocks = [p[...] for p in parts]
     width = blocks[0].shape[1]
     for s in range(n):
         pick = blocks[0]
         for k in range(1, n):
-            pick = jnp.where(lax.rem(me - k + n, n) == s, blocks[k], pick)
+            pick = jnp.where(source(me, k, n) == s, blocks[k], pick)
         normed_ref[:, s * width:(s + 1) * width] = pick
     rows = normed_ref[...].astype(F32)
     inv = lax.rsqrt(jnp.mean(rows * rows, axis=1, keepdims=True) + EPS)
     normed = (rows * inv * gain_ref[...]).astype(BF16)
     normed_ref[...] = normed
-    proj = lax.dot_general(normed, w_ref[...], NT, preferred_element_type=F32).astype(BF16)
+    side = jnp.concatenate([bcw_ref[...], dtw_ref[...]], axis=0)
+    both = lax.dot_general(normed, side, NT, preferred_element_type=F32).astype(BF16)
+    dt_ref[...] = both[:, bcw:bcw + heads].astype(F32)
+    proj = both[:, :bcw]
     proj_ref[...] = proj
     bc_ref[...] = silu(base_ref[...] + tap_ref[...] * proj.astype(F32)).astype(BF16)
 
 
-def in_kernel(hp, normed_ref, xw_ref, zw_ref, dtw_ref, base_ref, tap_ref, dtb_ref, rate_ref, skip_ref, own_ref,
-              live_ref, ow_ref, xproj_ref, g1_ref, g2_ref, g3_ref, u_ref, dec_ref, owv_ref, sem):
-    fetch = pltpu.make_async_copy(ow_ref, owv_ref, sem)
-    fetch.start()
+def terms(v):
+    high = v.astype(BF16)
+    rest = v - high.astype(F32)
+    mid = rest.astype(BF16)
+    return jnp.concatenate([high, mid, (rest - mid.astype(F32)).astype(BF16)], axis=0)
+
+
+def in_kernel(hp, _, normed_ref, xw_ref, zw_ref, base_ref, tap_ref, dt_ref, dtb_ref, rate_ref, skip_ref, own_ref,
+              live_ref, xproj_ref, g1_ref, g2_ref, g3_ref, u_ref, dec_ref):
     normed = normed_ref[...]
-    seqs = normed.shape[0]
+    xproj = jnp.dot(normed, xw_ref[...], preferred_element_type=F32).astype(BF16)
+    xproj_ref[...] = xproj
+    seqs, heads = dt_ref.shape
     chans = xw_ref.shape[1]
-    heads = dtw_ref.shape[0]
     live = live_ref[:, :1] > 0.0
-    dt = lax.dot_general(normed, dtw_ref[...], NT, preferred_element_type=F32).astype(BF16).astype(F32)
-    dt = softplus(dt + dtb_ref[...])
+    dt = softplus(dt_ref[...] + dtb_ref[...])
     decay = jnp.exp(-dt * jnp.exp(rate_ref[...]))
     spread = (lax.broadcasted_iota(jnp.int32, (heads, chans), 1) // hp
-              == lax.broadcasted_iota(jnp.int32, (heads, chans), 0)).astype(F32)
-    wide = jnp.concatenate([dt, decay, jnp.broadcast_to(skip_ref[...], dt.shape)], axis=0)
-    wide = jnp.dot(wide, spread, preferred_element_type=F32, precision=lax.Precision.HIGHEST)
-    dt_w, dec_w, skip_w = wide[:seqs], wide[seqs:2 * seqs], wide[2 * seqs:]
-    kept = jnp.where(live, decay, 1.0)
-    kept_slot = lax.dot_general(kept, own_ref[...], TN, preferred_element_type=F32, precision=lax.Precision.HIGHEST)
+              == lax.broadcasted_iota(jnp.int32, (heads, chans), 0)).astype(BF16)
+    rows = 2 * seqs + 16
+    wide = jnp.concatenate([dt, decay, jnp.broadcast_to(skip_ref[...], (16, heads))], axis=0)
+    wide = jnp.dot(terms(wide), spread, preferred_element_type=F32)
+    wide = wide[:rows] + wide[rows:2 * rows] + wide[2 * rows:]
+    dt_w, dec_w, skip_w = wide[:seqs], wide[seqs:2 * seqs], wide[2 * seqs:2 * seqs + 1]
+    own_b = own_ref[...].astype(BF16)
+    kept = lax.dot_general(terms(jnp.where(live, decay, 1.0)), jnp.concatenate([own_b] * 3, axis=0), TN,
+                           preferred_element_type=F32)
     for s in range(seqs):
-        dec_ref[s] = jnp.broadcast_to(kept_slot[:, s:s + 1], (heads, dec_ref.shape[2]))
-    xproj = jnp.dot(normed, xw_ref[...], preferred_element_type=F32).astype(BF16)
-    xproj_ref[...] = xproj
+        dec_ref[s] = jnp.broadcast_to(kept[:, s:s + 1], (heads, dec_ref.shape[2]))
     x = silu(base_ref[...] + tap_ref[...] * xproj.astype(F32)).astype(BF16).astype(F32)
     u = dt_w * x
+    live_u = jnp.where(live, u, 0.0)
+    high = live_u.astype(BF16)
+    u_slot = lax.dot_general(jnp.concatenate([own_b, own_b], axis=0),
+                             jnp.concatenate([high, (live_u - high.astype(F32)).astype(BF16)], axis=0), TN,
+                             preferred_element_type=F32)
+    u_ref[...] = u_slot.T
     zproj = jnp.dot(normed, zw_ref[...], preferred_element_type=F32).astype(BF16)
     gate = silu(zproj.astype(F32))
     g1_ref[...] = gate * dec_w
     g2_ref[...] = gate * u
     g3_ref[...] = gate * (skip_w * x)
-    u = jnp.where(live, u, 0.0)
-    high = u.astype(BF16)
-    low = (u - high.astype(F32)).astype(BF16)
-    own_b = own_ref[...].astype(BF16)
-    u_slot = (lax.dot_general(own_b, high, TN, preferred_element_type=F32)
-              + lax.dot_general(own_b, low, TN, preferred_element_type=F32))
-    u_ref[...] = u_slot.T
-    fetch.wait()
+
+
+def early(seqs):
+    return range(0, seqs, 2)
+
+
+def step_slot(s, dst, state_ref, u_ref, dec_ref, b_slot):
+    heads = dec_ref.shape[1]
+    hp = state_ref.shape[1] // heads
+    for h in range(heads):
+        rows = slice(h * hp, (h + 1) * hp)
+        dst[rows, :] = state_ref[s, rows, :] * dec_ref[s, h:h + 1, :] + u_ref[rows, s:s + 1] * b_slot[s:s + 1]
 
 
 def out_kernel(n, *refs):
     parts, refs = refs[:n], refs[n:]
-    state_ref, own_ref, g1_ref, g2_ref, g3_ref, gain_ref, w_ref = refs[:7]
-    sends, (own_sum_ref, bcf_ref, stage) = refs[7:7 + n - 1], refs[7 + n - 1:]
+    state_ref, own_ref, g1_ref, g2_ref, g3_ref, gain_ref, w_ref, u_ref, dec_ref = refs[:9]
+    sends, (own_sum_ref, bcf_ref, next_ref, stage, ring, sems) = refs[9:9 + n - 1], refs[9 + n - 1:]
     me = lax.axis_index("tp")
     seqs = g1_ref.shape[0]
     ns = state_ref.shape[2]
@@ -166,13 +185,19 @@
     for s in range(n):
         pick = blocks[0]
         for k in range(1, n):
-            pick = jnp.where(lax.rem(me - k + n, n) == s, blocks[k], pick)
+            pick = jnp.where(source(me, k, n) == s, blocks[k], pick)
         bcf_ref[:, s * width:(s + 1) * width] = pick
     own = own_ref[...] > 0.5
     b_rows, c_rows = bcf_ref[:, :ns].astype(F32), bcf_ref[:, ns:].astype(F32)
     dot_bc = jnp.sum(b_rows * c_rows, axis=1, keepdims=True)
-    y = None
+    b_slot = lax.dot_general(own_ref[...].astype(BF16), bcf_ref[:, :ns], TN, preferred_element_type=F32)
+    y, copies = None, []
     for s in range(0, seqs, 2):
+        if s in early(seqs):
+            at = len(copies)
+            step_slot(s, ring.at[at], state_ref, u_ref, dec_ref, b_slot)
+            copies.append(pltpu.make_async_copy(ring.at[at], next_ref.at[s], sems.at[at]))
+            copies[-1].start()
         pair = [jnp.where(own[:, t:t + 1], c_rows, 0.0).astype(BF16) for t in (s, s + 1)]
         both = jnp.concatenate([state_ref[s].astype(BF16), state_ref[s + 1].astype(BF16)], axis=1)
         term = lax.dot_general(jnp.concatenate(pair, axis=1), both, NT, preferred_element_type=F32)
@@ -189,40 +214,30 @@
         stage[d, :, width:] = tail
     own_sum_ref[...] = stage[me]
     for k in range(1, n):
-        sends[k - 1][...] = stage[lax.rem(me + k, n)].astype(BF16)
-
-
-def state_kernel(state_ref, u_ref, dec_ref, bcf_ref, own_ref, live_own_ref, xst_ref, xproj_ref, bcst_ref, bcproj_ref,
+        sends[k - 1][...] = stage[partner(me, k, n)].astype(BF16)
+    for copy in copies:
+        copy.wait()
+
+
+def state_kernel(_, state_ref, u_ref, dec_ref, bcf_ref, own_ref, live_own_ref, xst_ref, xproj_ref, bcst_ref, bcproj_ref,
                  next_ref, xnext_ref, bcnext_ref, ring, xkeep, bckeep, sems, pool_sems):
     seqs, chans, ns = state_ref.shape
-    heads = dec_ref.shape[1]
-    hp = chans // heads
     b_slot = lax.dot_general(own_ref[...].astype(BF16), bcf_ref[:, :ns], TN, preferred_element_type=F32)
-    depth = ring.shape[0]
-
-    def copy(s):
-        return pltpu.make_async_copy(ring.at[s % depth], next_ref.at[s], sems.at[s % depth])
-
-    for s in range(seqs):
-        if s >= depth:
-            copy(s - depth).wait()
-        for h in range(heads):
-            rows = slice(h * hp, (h + 1) * hp)
-            ring[s % depth, rows, :] = (
-                state_ref[s, rows, :] * dec_ref[s, h:h + 1, :] + u_ref[rows, s:s + 1] * b_slot[s:s + 1]
-            )
-        copy(s).start()
-        if s == seqs // 4:
+    late = [s for s in range(seqs) if s not in early(seqs)]
+    copies = []
+    for at, s in enumerate(late):
+        step_slot(s, ring.at[at], state_ref, u_ref, dec_ref, b_slot)
+        copies.append(pltpu.make_async_copy(ring.at[at], next_ref.at[s], sems.at[at]))
+        copies[-1].start()
+        if at == len(late) // 2:
             shift_state(xst_ref, xproj_ref[...], live_own_ref[...], xkeep)
             shift_state(bcst_ref, bcproj_ref[...], live_own_ref[...], bckeep)
             pools = [pltpu.make_async_copy(xkeep, xnext_ref, pool_sems.at[0]),
                      pltpu.make_async_copy(bckeep, bcnext_ref, pool_sems.at[1])]
             for pool in pools:
                 pool.start()
-    for s in range(max(0, seqs - depth), seqs):
-        copy(s).wait()
-    for pool in pools:
-        pool.wait()
+    for copy in copies + pools:
+        copy.wait()
 
 
 def final_kernel(chans, hid_ref, live_ref, own_ref, *refs):
@@ -242,21 +257,32 @@
 HB = pl.BlockSpec(memory_space=pltpu.HBM)
 
 
-def call(kernel, name, out, ins, args, outs=None, scratch=(), flops=1e6, moved=1e5, mib=4):
+def call(kernel, name, out, ins, args, outs=None, scratch=(), flops=1e6, moved=1e5, mib=4, alias=None):
     return pl.pallas_call(
         kernel,
         out_shape=out,
         in_specs=ins,
         out_specs=tuple(outs or [VM] * len(out)),
         scratch_shapes=list(scratch),
+        input_output_aliases=alias or {},
         name=name,
         compiler_params=pltpu.CompilerParams(vmem_limit_bytes=mib * 2 ** 20),
         cost_estimate=pl.CostEstimate(flops=int(flops), bytes_accessed=int(moved), transcendentals=0),
     )(*args)
 
 
+def partner(i, k, n):
+    return i ^ k if n & (n - 1) == 0 else lax.rem(i + k, n)
+
+
+def source(i, k, n):
+    return i ^ k if n & (n - 1) == 0 else lax.rem(i - k + n, n)
+
+
 def spread_out(values, n):
-    return [lax.ppermute(v, "tp", [(i, (i + k) % n) for i in range(n)]) for k, v in enumerate(values, 1)]
+    pairs = n & (n - 1) == 0
+    return [lax.ppermute(v, "tp", [(i, i ^ k if pairs else (i + k) % n) for i in range(n)])
+            for k, v in enumerate(values, 1)]
 
 
 def shards(hidden, in_gain, z_weight, x_weight, bc_weight, dt_weight, conv_x_weight, conv_x_bias, conv_bc_weight,
@@ -284,29 +310,32 @@
          like(src[6]), sds((seqs, bcw), F32), sds((1, bcw), F32), like(src[9]), sds((seqs, chans), F32),
          sds((1, chans), F32), like(src[12]), like(src[13]), like(src[14]), sds((seqs, 128), F32)),
         [HB] * len(src), tuple(map(pinned, src)), scratch=[*held.values(), pltpu.SemaphoreType.DMA((len(src),))], flops=4e6, moved=1e6)
-    normed, bc_own, bcproj = call(
+    normed, bc_own, bcproj, dt = call(
         functools.partial(bc_kernel, n), "bc",
-        (sds((seqs, n * width), BF16), sds((seqs, bcw), BF16), sds((seqs, bcw), BF16)),
-        [VM] * (n + 5), (*parts, gain, state, bcw_v, bcbase, bctap), flops=4e6)
+        (sds((seqs, n * width), BF16), sds((seqs, bcw), BF16), sds((seqs, bcw), BF16),
+         sds((seqs, heads), F32)),
+        [VM] * (n + 5), (*parts, gain, bcw_v, dtw_v, bcbase, bctap), flops=4e6)
     bc_parts = [bc_own] + spread_out([bc_own] * (n - 1), n)
     wide = sds((seqs, chans), F32)
-    xproj, g1, g2, g3, u, dec, out_w = call(
+    xproj, g1, g2, g3, u, dec = call(
         functools.partial(in_kernel, hp), "proj",
-        (sds((seqs, chans), BF16), wide, wide, wide, sds((chans, seqs), F32), sds((seqs, heads, 128), F32),
-         like(out_weight)),
-        [VM] * 11 + [HB], (normed, x_weight, z_weight, dtw_v, xbase, xtap, dtb, rate, skip, own, live, pinned(out_weight)),
-        scratch=[pltpu.SemaphoreType.DMA], flops=1e6, moved=1e5)
-    *sends, own_sum, bcf = call(
+        (sds((seqs, chans), BF16), wide, wide, wide, sds((chans, seqs), F32), sds((seqs, heads, 128), F32)),
+        [VM] * 12, (state, normed, x_weight, z_weight, xbase, xtap, dt, dtb, rate, skip, own, live))
+    count = len(early(seqs))
+    *sends, own_sum, bcf, begun = call(
         functools.partial(out_kernel, n), "out",
-        (*[sds((seqs, width + 128), BF16)] * (n - 1), sds((seqs, width + 128), F32), sds((seqs, n * bcw), BF16)),
-        [VM] * (n + 7), (*bc_parts, state, own, g1, g2, g3, ngain, out_w),
-        scratch=[pltpu.VMEM((n, seqs, width + 128), F32)], flops=2e8, moved=14e6, mib=12)
+        (*[sds((seqs, width + 128), BF16)] * (n - 1), sds((seqs, width + 128), F32), sds((seqs, n * bcw), BF16),
+         like(state)),
+        [VM] * (n + 9), (*bc_parts, state, own, g1, g2, g3, ngain, out_weight, u, dec), outs=(VM,) * (n + 1) + (HB,),
+        scratch=[pltpu.VMEM((n, seqs, width + 128), F32), pltpu.VMEM((count, chans, ns), F32),
+                 pltpu.SemaphoreType.DMA((count,))], flops=2e8, moved=14e6, mib=12)
     got = spread_out(sends, n)
     fresh, x_next, bc_next = call(
-        state_kernel, "state", (like(state), like(xst), like(bcst)), [VM] * 10,
-        (state, u, dec, bcf, own, live_own, xst, xproj, bcst, bcproj), outs=(HB, HB, HB),
-        scratch=[pltpu.VMEM((DEPTH, chans, ns), F32), pltpu.VMEM(xst.shape, BF16), pltpu.VMEM(bcst.shape, BF16),
-                 pltpu.SemaphoreType.DMA((DEPTH,)), pltpu.SemaphoreType.DMA((2,))], flops=2e8, moved=14e6, mib=12)
+        state_kernel, "state", (like(state), like(xst), like(bcst)), [HB] + [VM] * 10,
+        (begun, state, u, dec, bcf, own, live_own, xst, xproj, bcst, bcproj), outs=(HB, HB, HB),
+        scratch=[pltpu.VMEM((seqs - count, chans, ns), F32), pltpu.VMEM(xst.shape, BF16), pltpu.VMEM(bcst.shape, BF16),
+                 pltpu.SemaphoreType.DMA((seqs - count,)), pltpu.SemaphoreType.DMA((2,))], flops=2e8, moved=14e6, mib=12,
+        alias={0: 0})
     layer_out, = call(functools.partial(final_kernel, chans * n), "final", (like(hidden),), [VM] * (n + 2),
                       (hid, live, own_sum, *got))
     return (layer_out, x_next.transpose(1, 0, 2), bc_next.transpose(1, 0, 2), fresh.reshape(ssm_state.shape))

time: 24.6 us -> 21.6 us (0.88)
  Pallas kernels: 14.3 us -> 12.6 us
  starting transfers between devices: 8.16 us -> 6.96 us
    pallas_call x7, Pallas kernels: 14.3 us -> 12.6 us  [call(): pl.pallas_call(kernel, out_shape=out, in_specs=ins, out_specs=tuple(outs...]
    ppermute x9, starting transfers between devices: 8.16 us -> 6.96 us  [spread_out(): lax.ppermute(v, 'tp', [(i, i ^ k if pairs else (i + k) % n) for i in rang...]
  transfers between devices with their start and end apart: 9 -> 9, of which waited for: 3 -> 2; matrix products, arithmetic and copies ran while one was open for 0% -> 0% of each run, Pallas kernels for 39% -> 34%
where the time goes in v3:
time: 21.6 us; the launch traced here: 21.5 us
  Pallas kernels  12.6 us (58%)
  starting transfers between devices  6.96 us (32%)
  waiting for transfers between devices  1.13 us (5%)
  between operations  0.78 us (4%)
    pallas_call x7, Pallas kernels, call(): pl.pallas_call(kernel, out_shape=out, in_specs=ins, out_specs=tuple(outs...  12.6 us
    ppermute x9, starting transfers between devices, spread_out(): lax.ppermute(v, 'tp', [(i, i ^ k if pairs else (i + k) % n) for i in rang...  6.96 us
    ppermute x9, waiting for transfers between devices, spread_out(): lax.ppermute(v, 'tp', [(i, i ^ k if pairs else (i + k) % n) for i in rang...  1.13 us
  transfers between devices with their start and end apart: 9, of which 2 were waited for; matrix products, arithmetic and copies ran while one was open for 0% of the time, Pallas kernels for 34%

profile of v3, /device:TPU:0, one launch (start us, length us, event | category | flops | bytes accessed | tf_op | source)
XLA Modules:
  0.0 21.5 jit_solution(3733849141509287005)
XLA Ops:
  0.7 0.9 %load.1.refs_0_.hid_ref = bf16[16,640]{1,0:T(8,128)(2,1)S(1)} custom-call(bf16[16,640]{1,0:T(8,128)(2,1)} %src_ref.1), custom_call_target="tpu_custom_call" | custom-call | flops 20000000000 | bytes 100000 | tf_op jit(solution)/shard_map/load/pallas_call | solution.py:261
  1.6 2.5 %collective-permute-start.2 = (bf16[16,640]{1,0:T(8,128)(2,1)S(1)}, bf16[16,640]{1,0:T(8,128)(2,1)S(1)}, u32[]{:S(2)}, u32[]{:S(2)}) collective-permute-start(bf16[16,640]{1,0:T(8,128)(2,1)S(1)} %load.1.refs_0_.hid_ref), channel_id=1, source_target_pairs={{0,12},{4,8},{8,4},{12,0},{1,13},{5,9},{9,5},{13,1},{2,14},{6,10},... | collective-permute-start | bytes 61448 | tf_op jit(solution)/shard_map/ppermute | solution.py:284
  4.0 0.6 %collective-permute-start.1 = (bf16[16,640]{1,0:T(8,128)(2,1)S(1)}, bf16[16,640]{1,0:T(8,128)(2,1)S(1)}, u32[]{:S(2)}, u32[]{:S(2)}) collective-permute-start(bf16[16,640]{1,0:T(8,128)(2,1)S(1)} %load.1.refs_0_.hid_ref), channel_id=1, source_target_pairs={{0,8},{4,12},{8,0},{12,4},{1,9},{5,13},{9,1},{13,5},{2,10},{6,14},... | collective-permute-start | bytes 61448 | tf_op jit(solution)/shard_map/ppermute | solution.py:284
  4.7 0.0 collective-permute-start
  4.7 2.1 %prep.1 = (f32[1,2560]{1,0:T(1,128)S(1)}, f32[1,1280]{1,0:T(1,128)S(1)}, f32[16,16]{1,0:T(8,128)S(1)}, bf16[16,16]{1,0:T(8,128)(2,1)S(1)}, bf16[64,2560]{1,0:T(8...) custom-call(f32[2560]{0:T(1024)} %refs_0_.1, ...), custom_call_target="tpu_custom_call" | custom-call | flops 4000000 | bytes 1000000 | tf_op jit(solution)/shard_map/prep/pallas_call | solution.py:261
  6.8 0.0 collective-permute-done.2.refs_3_
  6.8 1.0 %collective-permute-done.1.refs_2_ = bf16[16,640]{1,0:T(8,128)(2,1)S(1)} collective-permute-done((bf16[16,640]{1,0:T(8,128)(2,1)S(1)}, bf16[16,640]{1,0:T(8,128)(2,1)S(1)}, u32[]{:S(2)}, u32[]{:S(2)}) %collective-permute-start.1) | collective-permute-done | bytes 20512 | tf_op jit(solution)/shard_map/ppermute | solution.py:284
  7.8 0.0 collective-permute-done.refs_1_
  7.8 0.4 %bc.1 = (bf16[16,2560]{1,0:T(8,128)(2,1)S(1)}, bf16[16,64]{1,0:T(8,128)(2,1)S(1)}, bf16[16,64]{1,0:T(8,128)(2,1)S(1)}, f32[16,20]{1,0:T(8,128)S(1)}) custom-call(bf16[16,640]{1,0:T(8,128)(2,1)S(1)} %load.1.refs_0_.hid_ref, bf16[16,640]{1,0:T(8,128)(2,1)S(1)} %collective-permute-done.refs_1_, bf16[16,640]{1,0:T(8,128)(2,1)S(1)} %collective-permute-done.1.refs_2_, ...), custom_call_target="tpu_custom_call" | custom-call | flops 4000000 | bytes 100000 | tf_op jit(solution)/shard_map/bc/pallas_call | solution.py:261
  8.2 0.5 %collective-permute-start.5 = (bf16[16,64]{1,0:T(8,128)(2,1)S(1)}, bf16[16,64]{1,0:T(8,128)(2,1)S(1)}, u32[]{:S(2)}, u32[]{:S(2)}) collective-permute-start(bf16[16,64]{1,0:T(8,128)(2,1)S(1)} %get-tuple-element.45.refs_0_), channel_id=1, source_target_pairs={{0,12},{4,8},{8,4},{12,0},{1,13},{5,9},{9,5},{13,1},{2,14},{6,10},... | collective-permute-start | bytes 6152 | tf_op jit(solution)/shard_map/ppermute | solution.py:284
  8.7 0.7 %collective-permute-start.4 = (bf16[16,64]{1,0:T(8,128)(2,1)S(1)}, bf16[16,64]{1,0:T(8,128)(2,1)S(1)}, u32[]{:S(2)}, u32[]{:S(2)}) collective-permute-start(bf16[16,64]{1,0:T(8,128)(2,1)S(1)} %get-tuple-element.45.refs_0_), channel_id=1, source_target_pairs={{0,8},{4,12},{8,0},{12,4},{1,9},{5,13},{9,1},{13,5},{2,10},{6,14},... | collective-permute-start | bytes 6152 | tf_op jit(solution)/shard_map/ppermute | solution.py:284
  9.4 0.7 %collective-permute-start.3 = (bf16[16,64]{1,0:T(8,128)(2,1)S(1)}, bf16[16,64]{1,0:T(8,128)(2,1)S(1)}, u32[]{:S(2)}, u32[]{:S(2)}) collective-permute-start(bf16[16,64]{1,0:T(8,128)(2,1)S(1)} %get-tuple-element.45.refs_0_), channel_id=1, source_target_pairs={{0,4},{4,0},{8,12},{12,8},{1,5},{5,1},{9,13},{13,9},{2,6},{6,2},{1... | collective-permute-start | bytes 6152 | tf_op jit(solution)/shard_map/ppermute | solution.py:284
  10.1 2.4 %proj.1 = (bf16[16,1280]{1,0:T(8,128)(2,1)S(1)}, f32[16,1280]{1,0:T(8,128)S(1)}, f32[16,1280]{1,0:T(8,128)S(1)}, f32[16,1280]{1,0:T(8,128)S(1)}, f32[1280,16]{1,0:T(8,128)S(1)}, /*index=5*/f32[16,20,128]{2,1,0:T(8,128)S(1)}) custom-call(f32[16,1280,128]{2,1,0:T(8,128)S(1)} %bitcast.13, bf16[16,2560]{1,0:T(8,128)(2,1)S(1)} %get-tuple-element.47.normed_ref, ...), custom_call_target="tpu_custom_call" | custom-call | flops 1000000 | bytes 100000 | tf_op jit(solution)/shard_map/proj/pallas_call | solution.py:261
  12.6 0.0 collective-permute-done.5.refs_3_
  12.6 0.0 collective-permute-done.4.refs_2_
  12.6 0.0 collective-permute-done.3.refs_1_
  12.6 3.2 %out.1 = (bf16[16,768]{1,0:T(8,128)(2,1)S(1)}, bf16[16,768]{1,0:T(8,128)(2,1)S(1)}, bf16[16,768]{1,0:T(8,128)(2,1)S(1)}, f32[16,768]{1,0:T(8,128)S(1)}, bf16[16,...) custom-call(bf16[16,64]{1,0:T(8,128)(2,1)S(1)} %get-tuple-element.45.refs_0_, ...), custom_call_target="tpu_custom_call" | custom-call | flops 200000000 | bytes 14000000 | tf_op jit(solution)/shard_map/out/pallas_call | solution.py:261
  15.8 0.1 collective-permute-start.6
  15.9 1.6 %collective-permute-start.7 = (bf16[16,768]{1,0:T(8,128)(2,1)S(1)}, bf16[16,768]{1,0:T(8,128)(2,1)S(1)}, u32[]{:S(2)}, u32[]{:S(2)}) collective-permute-start(bf16[16,768]{1,0:T(8,128)(2,1)S(1)} %get-tuple-element.62), channel_id=1, source_target_pairs={{0,8},{4,12},{8,0},{12,4},{1,9},{5,13},{9,1},{13,5},{2,10},{6,14},... | collective-permute-start | bytes 73736 | tf_op jit(solution)/shard_map/ppermute | solution.py:284
  17.4 0.3 %collective-permute-start.8 = (bf16[16,768]{1,0:T(8,128)(2,1)S(1)}, bf16[16,768]{1,0:T(8,128)(2,1)S(1)}, u32[]{:S(2)}, u32[]{:S(2)}) collective-permute-start(bf16[16,768]{1,0:T(8,128)(2,1)S(1)} %get-tuple-element.63), channel_id=1, source_target_pairs={{0,12},{4,8},{8,4},{12,0},{1,13},{5,9},{9,5},{13,1},{2,14},{6,10},... | collective-permute-start | bytes 73736 | tf_op jit(solution)/shard_map/ppermute | solution.py:284
  17.7 2.8 %state.1 = (f32[16,1280,128]{2,1,0:T(8,128)}, bf16[3,16,1280]{2,1,0:T(8,128)(2,1)}, bf16[3,16,64]{2,1,0:T(8,128)(2,1)}) custom-call(f32[16,1280,128]{2,1,0:T(8,128)} %get-tuple-element.64._, f32[16,1280,128]{2,1,0:T(8,128)S(1)} %bitcast.15, f32[1280,16]{1,0:T(8,128)S(1)} %get-tuple-element.58.refs_11_.u_ref, ...), custom_call_target="tpu_custom_call", output_to_operand_aliasing={{0}: (0, {})} | custom-call | flops 200000000 | bytes 14000000 | tf_op jit(solution)/shard_map/state/pallas_call | solution.py:261
  20.6 0.0 collective-permute-done.6.refs_0_
  20.6 0.1 collective-permute-done.8.refs_2_
  20.7 0.8 %final.1 = bf16[16,640]{1,0:T(8,128)(2,1)} custom-call(bf16[16,640]{1,0:T(8,128)(2,1)S(1)} %load.1.refs_0_.hid_ref, f32[16,128]{1,0:T(8,128)S(1)} %get-tuple-element.39.live_ref, f32[16,768]{1,0:T(8,128)S(1)} %get-tuple-element.60.own_ref, bf16[16,768]{1,0:T(8,128)(2,1)S(1)} %collective-permute-done.6.refs_0_, ...), custom_call_target="tpu_custom_call" | custom-call | flops 1000000 | bytes 100000 | tf_op jit(solution)/shard_map/final/pallas_call | solution.py:261
  (12 shorter events, 0.0 us)
Async XLA Ops:
  0.6 9.5 %copy-start = (f32[16,20,64,128]{3,2,1,0:T(8,128)S(1)}, f32[16,20,64,128]{3,2,1,0:T(8,128)}, u32[]{:S(2)}) copy-start(f32[16,20,64,128]{3,2,1,0:T(8,128)} %param.35) | copy-start | bytes 31457284
  0.6 9.5 %copy-start.1 = (bf16[2560,1280]{1,0:T(8,128)(2,1)S(1)}, bf16[2560,1280]{1,0:T(8,128)(2,1)}, u32[]{:S(2)}) copy-start(bf16[2560,1280]{1,0:T(8,128)(2,1)} %xw_ref.1) | copy-start | bytes 19660804
  0.7 9.5 %copy-start.2 = (bf16[2560,1280]{1,0:T(8,128)(2,1)S(1)}, bf16[2560,1280]{1,0:T(8,128)(2,1)}, u32[]{:S(2)}) copy-start(bf16[2560,1280]{1,0:T(8,128)(2,1)} %zw_ref.1) | copy-start | bytes 19660804
  1.6 5.2 %collective-permute-start.2 = (bf16[16,640]{1,0:T(8,128)(2,1)S(1)}, bf16[16,640]{1,0:T(8,128)(2,1)S(1)}, u32[]{:S(2)}, u32[]{:S(2)}) collective-permute-start(bf16[16,640]{1,0:T(8,128)(2,1)S(1)} %load.1.refs_0_.hid_ref), channel_id=1, source_target_pairs={{0,12},{4,8},{8,4},{12,0},{1,13},{5,9},{9,5},{13,1},{2,14},{6,10},... | collective-permute-start | bytes 61448 | tf_op jit(solution)/shard_map/ppermute | solution.py:284
  4.0 3.8 %collective-permute-start.1 = (bf16[16,640]{1,0:T(8,128)(2,1)S(1)}, bf16[16,640]{1,0:T(8,128)(2,1)S(1)}, u32[]{:S(2)}, u32[]{:S(2)}) collective-permute-start(bf16[16,640]{1,0:T(8,128)(2,1)S(1)} %load.1.refs_0_.hid_ref), channel_id=1, source_target_pairs={{0,8},{4,12},{8,0},{12,4},{1,9},{5,13},{9,1},{13,5},{2,10},{6,14},... | collective-permute-start | bytes 61448 | tf_op jit(solution)/shard_map/ppermute | solution.py:284
  4.7 3.1 %collective-permute-start = (bf16[16,640]{1,0:T(8,128)(2,1)S(1)}, bf16[16,640]{1,0:T(8,128)(2,1)S(1)}, u32[]{:S(2)}, u32[]{:S(2)}) collective-permute-start(bf16[16,640]{1,0:T(8,128)(2,1)S(1)} %load.1.refs_0_.hid_ref), channel_id=1, source_target_pairs={{0,4},{4,0},{8,12},{12,8},{1,5},{5,1},{9,13},{13,9},{2,6},{6,2},{1... | collective-permute-start | bytes 61448 | tf_op jit(solution)/shard_map/ppermute | solution.py:284
  4.7 7.9 %slice-start = ((s8[6553600]{0:T(1024)(128)(4,1)}), s8[4194304]{0:T(1024)(128)(4,1)S(1)}, s32[]{:S(2)}) async-start(s8[6553600]{0:T(1024)(128)(4,1)} %bitcast.16), calls=%async_computation | async-start | bytes 8388608
  8.2 4.3 %collective-permute-start.5 = (bf16[16,64]{1,0:T(8,128)(2,1)S(1)}, bf16[16,64]{1,0:T(8,128)(2,1)S(1)}, u32[]{:S(2)}, u32[]{:S(2)}) collective-permute-start(bf16[16,64]{1,0:T(8,128)(2,1)S(1)} %get-tuple-element.45.refs_0_), channel_id=1, source_target_pairs={{0,12},{4,8},{8,4},{12,0},{1,13},{5,9},{9,5},{13,1},{2,14},{6,10},... | collective-permute-start | bytes 6152 | tf_op jit(solution)/shard_map/ppermute | solution.py:284
  8.7 3.8 %collective-permute-start.4 = (bf16[16,64]{1,0:T(8,128)(2,1)S(1)}, bf16[16,64]{1,0:T(8,128)(2,1)S(1)}, u32[]{:S(2)}, u32[]{:S(2)}) collective-permute-start(bf16[16,64]{1,0:T(8,128)(2,1)S(1)} %get-tuple-element.45.refs_0_), channel_id=1, source_target_pairs={{0,8},{4,12},{8,0},{12,4},{1,9},{5,13},{9,1},{13,5},{2,10},{6,14},... | collective-permute-start | bytes 6152 | tf_op jit(solution)/shard_map/ppermute | solution.py:284
  9.4 3.2 %collective-permute-start.3 = (bf16[16,64]{1,0:T(8,128)(2,1)S(1)}, bf16[16,64]{1,0:T(8,128)(2,1)S(1)}, u32[]{:S(2)}, u32[]{:S(2)}) collective-permute-start(bf16[16,64]{1,0:T(8,128)(2,1)S(1)} %get-tuple-element.45.refs_0_), channel_id=1, source_target_pairs={{0,4},{4,0},{8,12},{12,8},{1,5},{5,1},{9,13},{13,9},{2,6},{6,2},{1... | collective-permute-start | bytes 6152 | tf_op jit(solution)/shard_map/ppermute | solution.py:284
  10.1 2.5 %slice-start.1 = ((s8[6553600]{0:T(1024)(128)(4,1)}), s8[2359296]{0:T(1024)(128)(4,1)S(1)}, s32[]{:S(2)}) async-start(s8[6553600]{0:T(1024)(128)(4,1)} %bitcast.16), calls=%async_computation.1 | async-start | bytes 4718592
  15.8 4.8 %collective-permute-start.6 = (bf16[16,768]{1,0:T(8,128)(2,1)S(1)}, bf16[16,768]{1,0:T(8,128)(2,1)S(1)}, u32[]{:S(2)}, u32[]{:S(2)}) collective-permute-start(bf16[16,768]{1,0:T(8,128)(2,1)S(1)} %get-tuple-element.61), channel_id=1, source_target_pairs={{0,4},{4,0},{8,12},{12,8},{1,5},{5,1},{9,13},{13,9},{2,6},{6,2},{1... | collective-permute-start | bytes 73736 | tf_op jit(solution)/shard_map/ppermute | solution.py:284
  15.9 4.7 %collective-permute-start.7 = (bf16[16,768]{1,0:T(8,128)(2,1)S(1)}, bf16[16,768]{1,0:T(8,128)(2,1)S(1)}, u32[]{:S(2)}, u32[]{:S(2)}) collective-permute-start(bf16[16,768]{1,0:T(8,128)(2,1)S(1)} %get-tuple-element.62), channel_id=1, source_target_pairs={{0,8},{4,12},{8,0},{12,4},{1,9},{5,13},{9,1},{13,5},{2,10},{6,14},... | collective-permute-start | bytes 73736 | tf_op jit(solution)/shard_map/ppermute | solution.py:284
  17.4 3.3 %collective-permute-start.8 = (bf16[16,768]{1,0:T(8,128)(2,1)S(1)}, bf16[16,768]{1,0:T(8,128)(2,1)S(1)}, u32[]{:S(2)}, u32[]{:S(2)}) collective-permute-start(bf16[16,768]{1,0:T(8,128)(2,1)S(1)} %get-tuple-element.63), channel_id=1, source_target_pairs={{0,12},{4,8},{8,4},{12,0},{1,13},{5,9},{9,5},{13,1},{2,14},{6,10},... | collective-permute-start | bytes 73736 | tf_op jit(solution)/shard_map/ppermute | solution.py:284

commit v4 on v3

--- a/solution.py
+++ b/solution.py
@@ -124,7 +124,7 @@
     return jnp.concatenate([high, mid, (rest - mid.astype(F32)).astype(BF16)], axis=0)
 
 
-def in_kernel(hp, _, normed_ref, xw_ref, zw_ref, base_ref, tap_ref, dt_ref, dtb_ref, rate_ref, skip_ref, own_ref,
+def in_kernel(hp, normed_ref, xw_ref, zw_ref, base_ref, tap_ref, dt_ref, dtb_ref, rate_ref, skip_ref, own_ref,
               live_ref, xproj_ref, g1_ref, g2_ref, g3_ref, u_ref, dec_ref):
     normed = normed_ref[...]
     xproj = jnp.dot(normed, xw_ref[...], preferred_element_type=F32).astype(BF16)
@@ -159,6 +159,10 @@
     g1_ref[...] = gate * dec_w
     g2_ref[...] = gate * u
     g3_ref[...] = gate * (skip_w * x)
+
+
+def hold_kernel(_, __, after_ref, own_ref, out_ref):
+    out_ref[...] = own_ref[...]
 
 
 def early(seqs):
@@ -320,13 +324,14 @@
     xproj, g1, g2, g3, u, dec = call(
         functools.partial(in_kernel, hp), "proj",
         (sds((seqs, chans), BF16), wide, wide, wide, sds((chans, seqs), F32), sds((seqs, heads, 128), F32)),
-        [VM] * 12, (state, normed, x_weight, z_weight, xbase, xtap, dt, dtb, rate, skip, own, live))
+        [VM] * 11, (normed, x_weight, z_weight, xbase, xtap, dt, dtb, rate, skip, own, live))
+    own_held, = call(hold_kernel, "hold", (like(own),), [VM] * 4, (state, out_weight, u, own))
     count = len(early(seqs))
     *sends, own_sum, bcf, begun = call(
         functools.partial(out_kernel, n), "out",
         (*[sds((seqs, width + 128), BF16)] * (n - 1), sds((seqs, width + 128), F32), sds((seqs, n * bcw), BF16),
          like(state)),
-        [VM] * (n + 9), (*bc_parts, state, own, g1, g2, g3, ngain, out_weight, u, dec), outs=(VM,) * (n + 1) + (HB,),
+        [VM] * (n + 9), (*bc_parts, state, own_held, g1, g2, g3, ngain, out_weight, u, dec), outs=(VM,) * (n + 1) + (HB,),
         scratch=[pltpu.VMEM((n, seqs, width + 128), F32), pltpu.VMEM((count, chans, ns), F32),
                  pltpu.SemaphoreType.DMA((count,))], flops=2e8, moved=14e6, mib=12)
     got = spread_out(sends, n)

time: 21.6 us -> 21.5 us (level)
    pallas_call x7 -> x8, Pallas kernels: 12.6 us -> 12.6 us  [call(): pl.pallas_call(kernel, out_shape=out, in_specs=ins, out_specs=tuple(outs...]
  transfers between devices with their start and end apart: 9 -> 9, of which waited for: 2 -> 1; matrix products, arithmetic and copies ran while one was open for 0% -> 0% of each run, Pallas kernels for 34% -> 34%
where the time goes in v4:
time: 21.5 us; the launch traced here: 21.4 us
  Pallas kernels  12.6 us (59%)
  starting transfers between devices  6.96 us (32%)
  waiting for transfers between devices  1.02 us (5%)
  between operations  0.79 us (4%)
    pallas_call x8, Pallas kernels, call(): pl.pallas_call(kernel, out_shape=out, in_specs=ins, out_specs=tuple(outs...  12.6 us
    ppermute x9, starting transfers between devices, spread_out(): lax.ppermute(v, 'tp', [(i, i ^ k if pairs else (i + k) % n) for i in rang...  6.96 us
    ppermute x9, waiting for transfers between devices, spread_out(): lax.ppermute(v, 'tp', [(i, i ^ k if pairs else (i + k) % n) for i in rang...  1.02 us
  transfers between devices with their start and end apart: 9, of which 1 were waited for; matrix products, arithmetic and copies ran while one was open for 0% of the time, Pallas kernels for 34%

profile of v4, /device:TPU:0, one launch (start us, length us, event | category | flops | bytes accessed | tf_op | source)
XLA Modules:
  0.0 21.4 jit_solution(13338867729964410020)
XLA Ops:
  0.7 0.9 %load.1.refs_0_.hid_ref = bf16[16,640]{1,0:T(8,128)(2,1)S(1)} custom-call(bf16[16,640]{1,0:T(8,128)(2,1)} %src_ref.1), custom_call_target="tpu_custom_call" | custom-call | flops 20000000000 | bytes 100000 | tf_op jit(solution)/shard_map/load/pallas_call | solution.py:265
  1.6 0.0 copy-start
  1.6 2.5 %collective-permute-start.2 = (bf16[16,640]{1,0:T(8,128)(2,1)S(1)}, bf16[16,640]{1,0:T(8,128)(2,1)S(1)}, u32[]{:S(2)}, u32[]{:S(2)}) collective-permute-start(bf16[16,640]{1,0:T(8,128)(2,1)S(1)} %load.1.refs_0_.hid_ref), channel_id=1, source_target_pairs={{0,12},{4,8},{8,4},{12,0},{1,13},{5,9},{9,5},{13,1},{2,14},{6,10},... | collective-permute-start | bytes 61448 | tf_op jit(solution)/shard_map/ppermute | solution.py:288
  4.0 0.6 %collective-permute-start.1 = (bf16[16,640]{1,0:T(8,128)(2,1)S(1)}, bf16[16,640]{1,0:T(8,128)(2,1)S(1)}, u32[]{:S(2)}, u32[]{:S(2)}) collective-permute-start(bf16[16,640]{1,0:T(8,128)(2,1)S(1)} %load.1.refs_0_.hid_ref), channel_id=1, source_target_pairs={{0,8},{4,12},{8,0},{12,4},{1,9},{5,13},{9,1},{13,5},{2,10},{6,14},... | collective-permute-start | bytes 61448 | tf_op jit(solution)/shard_map/ppermute | solution.py:288
  4.7 0.0 collective-permute-start
  4.7 2.1 %prep.1 = (f32[1,2560]{1,0:T(1,128)S(1)}, f32[1,1280]{1,0:T(1,128)S(1)}, f32[16,16]{1,0:T(8,128)S(1)}, bf16[16,16]{1,0:T(8,128)(2,1)S(1)}, bf16[64,2560]{1,0:T(8...) custom-call(f32[2560]{0:T(1024)} %refs_0_.1, ...), custom_call_target="tpu_custom_call" | custom-call | flops 4000000 | bytes 1000000 | tf_op jit(solution)/shard_map/prep/pallas_call | solution.py:265
  6.8 0.0 collective-permute-done.2.refs_3_
  6.8 1.0 %collective-permute-done.1.refs_2_ = bf16[16,640]{1,0:T(8,128)(2,1)S(1)} collective-permute-done((bf16[16,640]{1,0:T(8,128)(2,1)S(1)}, bf16[16,640]{1,0:T(8,128)(2,1)S(1)}, u32[]{:S(2)}, u32[]{:S(2)}) %collective-permute-start.1) | collective-permute-done | bytes 20512 | tf_op jit(solution)/shard_map/ppermute | solution.py:288
  7.8 0.0 collective-permute-done.refs_1_
  7.8 0.4 %bc.1 = (bf16[16,2560]{1,0:T(8,128)(2,1)S(1)}, bf16[16,64]{1,0:T(8,128)(2,1)S(1)}, bf16[16,64]{1,0:T(8,128)(2,1)S(1)}, f32[16,20]{1,0:T(8,128)S(1)}) custom-call(bf16[16,640]{1,0:T(8,128)(2,1)S(1)} %load.1.refs_0_.hid_ref, bf16[16,640]{1,0:T(8,128)(2,1)S(1)} %collective-permute-done.refs_1_, bf16[16,640]{1,0:T(8,128)(2,1)S(1)} %collective-permute-done.1.refs_2_, ...), custom_call_target="tpu_custom_call" | custom-call | flops 4000000 | bytes 100000 | tf_op jit(solution)/shard_map/bc/pallas_call | solution.py:265
  8.2 0.5 %collective-permute-start.5 = (bf16[16,64]{1,0:T(8,128)(2,1)S(1)}, bf16[16,64]{1,0:T(8,128)(2,1)S(1)}, u32[]{:S(2)}, u32[]{:S(2)}) collective-permute-start(bf16[16,64]{1,0:T(8,128)(2,1)S(1)} %get-tuple-element.45.refs_0_), channel_id=1, source_target_pairs={{0,12},{4,8},{8,4},{12,0},{1,13},{5,9},{9,5},{13,1},{2,14},{6,10},... | collective-permute-start | bytes 6152 | tf_op jit(solution)/shard_map/ppermute | solution.py:288
  8.7 0.7 %collective-permute-start.4 = (bf16[16,64]{1,0:T(8,128)(2,1)S(1)}, bf16[16,64]{1,0:T(8,128)(2,1)S(1)}, u32[]{:S(2)}, u32[]{:S(2)}) collective-permute-start(bf16[16,64]{1,0:T(8,128)(2,1)S(1)} %get-tuple-element.45.refs_0_), channel_id=1, source_target_pairs={{0,8},{4,12},{8,0},{12,4},{1,9},{5,13},{9,1},{13,5},{2,10},{6,14},... | collective-permute-start | bytes 6152 | tf_op jit(solution)/shard_map/ppermute | solution.py:288
  9.4 0.7 %collective-permute-start.3 = (bf16[16,64]{1,0:T(8,128)(2,1)S(1)}, bf16[16,64]{1,0:T(8,128)(2,1)S(1)}, u32[]{:S(2)}, u32[]{:S(2)}) collective-permute-start(bf16[16,64]{1,0:T(8,128)(2,1)S(1)} %get-tuple-element.45.refs_0_), channel_id=1, source_target_pairs={{0,4},{4,0},{8,12},{12,8},{1,5},{5,1},{9,13},{13,9},{2,6},{6,2},{1... | collective-permute-start | bytes 6152 | tf_op jit(solution)/shard_map/ppermute | solution.py:288
  10.1 2.4 %proj.1 = (bf16[16,1280]{1,0:T(8,128)(2,1)S(1)}, f32[16,1280]{1,0:T(8,128)S(1)}, f32[16,1280]{1,0:T(8,128)S(1)}, f32[16,1280]{1,0:T(8,128)S(1)}, f32[1280,16]{1,0:T(8,128)S(1)}, /*index=5*/f32[16,20,128]{2,1,0:T(8,128)S(1)}) custom-call(bf16[16,2560]{1,0:T(8,128)(2,1)S(1)} %get-tuple-element.46.normed_ref, bf16[2560,1280]{1,0:T(8,128)(2,1)S(1)} %copy-done.2, ...), custom_call_target="tpu_custom_call" | custom-call | flops 1000000 | bytes 100000 | tf_op jit(solution)/shard_map/proj/pallas_call | solution.py:265
  12.6 0.0 collective-permute-done.4.refs_2_
  12.6 0.0 collective-permute-done.3.refs_1_
  12.6 3.2 %out.1 = (bf16[16,768]{1,0:T(8,128)(2,1)S(1)}, bf16[16,768]{1,0:T(8,128)(2,1)S(1)}, bf16[16,768]{1,0:T(8,128)(2,1)S(1)}, f32[16,768]{1,0:T(8,128)S(1)}, bf16[16,...) custom-call(bf16[16,64]{1,0:T(8,128)(2,1)S(1)} %get-tuple-element.45.refs_0_, ...), custom_call_target="tpu_custom_call" | custom-call | flops 200000000 | bytes 14000000 | tf_op jit(solution)/shard_map/out/pallas_call | solution.py:265
  15.8 0.1 collective-permute-start.6
  15.9 1.2 %collective-permute-start.7 = (bf16[16,768]{1,0:T(8,128)(2,1)S(1)}, bf16[16,768]{1,0:T(8,128)(2,1)S(1)}, u32[]{:S(2)}, u32[]{:S(2)}) collective-permute-start(bf16[16,768]{1,0:T(8,128)(2,1)S(1)} %get-tuple-element.62), channel_id=1, source_target_pairs={{0,8},{4,12},{8,0},{12,4},{1,9},{5,13},{9,1},{13,5},{2,10},{6,14},... | collective-permute-start | bytes 73736 | tf_op jit(solution)/shard_map/ppermute | solution.py:288
  17.1 0.6 %collective-permute-start.8 = (bf16[16,768]{1,0:T(8,128)(2,1)S(1)}, bf16[16,768]{1,0:T(8,128)(2,1)S(1)}, u32[]{:S(2)}, u32[]{:S(2)}) collective-permute-start(bf16[16,768]{1,0:T(8,128)(2,1)S(1)} %get-tuple-element.63), channel_id=1, source_target_pairs={{0,12},{4,8},{8,4},{12,0},{1,13},{5,9},{9,5},{13,1},{2,14},{6,10},... | collective-permute-start | bytes 73736 | tf_op jit(solution)/shard_map/ppermute | solution.py:288
  17.7 2.8 %state.1 = (f32[16,1280,128]{2,1,0:T(8,128)}, bf16[3,16,1280]{2,1,0:T(8,128)(2,1)}, bf16[3,16,64]{2,1,0:T(8,128)(2,1)}) custom-call(f32[16,1280,128]{2,1,0:T(8,128)} %get-tuple-element.64._, f32[16,1280,128]{2,1,0:T(8,128)S(1)} %bitcast.15, f32[1280,16]{1,0:T(8,128)S(1)} %get-tuple-element.54.after_ref.refs_11_.u_ref, ...), custom_call_target="tpu_custom_call", output_to_operand_aliasing={{0}: (0, {})} | custom-call | flops 200000000 | bytes 14000000 | tf_op jit(solution)/shard_map/state/pallas_call | solution.py:265
  20.6 0.0 collective-permute-done.6.refs_0_
  20.6 0.0 collective-permute-done.7.refs_1_
  20.6 0.8 %final.1 = bf16[16,640]{1,0:T(8,128)(2,1)} custom-call(bf16[16,640]{1,0:T(8,128)(2,1)S(1)} %load.1.refs_0_.hid_ref, f32[16,128]{1,0:T(8,128)S(1)} %get-tuple-element.39.live_ref, f32[16,768]{1,0:T(8,128)S(1)} %get-tuple-element.60.own_ref, bf16[16,768]{1,0:T(8,128)(2,1)S(1)} %collective-permute-done.6.refs_0_, ...), custom_call_target="tpu_custom_call" | custom-call | flops 1000000 | bytes 100000 | tf_op jit(solution)/shard_map/final/pallas_call | solution.py:265
  (10 shorter events, 0.0 us)
Async XLA Ops:
  0.6 9.5 %copy-start.2 = (bf16[2560,1280]{1,0:T(8,128)(2,1)S(1)}, bf16[2560,1280]{1,0:T(8,128)(2,1)}, u32[]{:S(2)}) copy-start(bf16[2560,1280]{1,0:T(8,128)(2,1)} %xw_ref.1) | copy-start | bytes 19660804
  0.6 9.5 %copy-start.3 = (bf16[2560,1280]{1,0:T(8,128)(2,1)S(1)}, bf16[2560,1280]{1,0:T(8,128)(2,1)}, u32[]{:S(2)}) copy-start(bf16[2560,1280]{1,0:T(8,128)(2,1)} %zw_ref.1) | copy-start | bytes 19660804
  0.7 11.9 %copy-start.1 = (bf16[1280,2560]{1,0:T(8,128)(2,1)S(1)}, bf16[1280,2560]{1,0:T(8,128)(2,1)}, u32[]{:S(2)}) copy-start(bf16[1280,2560]{1,0:T(8,128)(2,1)} %refs_10_.3) | copy-start | bytes 19660804
  1.6 11.0 %copy-start = (f32[16,20,64,128]{3,2,1,0:T(8,128)S(1)}, f32[16,20,64,128]{3,2,1,0:T(8,128)}, u32[]{:S(2)}) copy-start(f32[16,20,64,128]{3,2,1,0:T(8,128)} %param.35) | copy-start | bytes 31457284
  1.6 5.2 %collective-permute-start.2 = (bf16[16,640]{1,0:T(8,128)(2,1)S(1)}, bf16[16,640]{1,0:T(8,128)(2,1)S(1)}, u32[]{:S(2)}, u32[]{:S(2)}) collective-permute-start(bf16[16,640]{1,0:T(8,128)(2,1)S(1)} %load.1.refs_0_.hid_ref), channel_id=1, source_target_pairs={{0,12},{4,8},{8,4},{12,0},{1,13},{5,9},{9,5},{13,1},{2,14},{6,10},... | collective-permute-start | bytes 61448 | tf_op jit(solution)/shard_map/ppermute | solution.py:288
  4.0 3.8 %collective-permute-start.1 = (bf16[16,640]{1,0:T(8,128)(2,1)S(1)}, bf16[16,640]{1,0:T(8,128)(2,1)S(1)}, u32[]{:S(2)}, u32[]{:S(2)}) collective-permute-start(bf16[16,640]{1,0:T(8,128)(2,1)S(1)} %load.1.refs_0_.hid_ref), channel_id=1, source_target_pairs={{0,8},{4,12},{8,0},{12,4},{1,9},{5,13},{9,1},{13,5},{2,10},{6,14},... | collective-permute-start | bytes 61448 | tf_op jit(solution)/shard_map/ppermute | solution.py:288
  4.7 3.1 %collective-permute-start = (bf16[16,640]{1,0:T(8,128)(2,1)S(1)}, bf16[16,640]{1,0:T(8,128)(2,1)S(1)}, u32[]{:S(2)}, u32[]{:S(2)}) collective-permute-start(bf16[16,640]{1,0:T(8,128)(2,1)S(1)} %load.1.refs_0_.hid_ref), channel_id=1, source_target_pairs={{0,4},{4,0},{8,12},{12,8},{1,5},{5,1},{9,13},{13,9},{2,6},{6,2},{1... | collective-permute-start | bytes 61448 | tf_op jit(solution)/shard_map/ppermute | solution.py:288
  8.2 4.3 %collective-permute-start.5 = (bf16[16,64]{1,0:T(8,128)(2,1)S(1)}, bf16[16,64]{1,0:T(8,128)(2,1)S(1)}, u32[]{:S(2)}, u32[]{:S(2)}) collective-permute-start(bf16[16,64]{1,0:T(8,128)(2,1)S(1)} %get-tuple-element.45.refs_0_), channel_id=1, source_target_pairs={{0,12},{4,8},{8,4},{12,0},{1,13},{5,9},{9,5},{13,1},{2,14},{6,10},... | collective-permute-start | bytes 6152 | tf_op jit(solution)/shard_map/ppermute | solution.py:288
  8.7 3.9 %collective-permute-start.4 = (bf16[16,64]{1,0:T(8,128)(2,1)S(1)}, bf16[16,64]{1,0:T(8,128)(2,1)S(1)}, u32[]{:S(2)}, u32[]{:S(2)}) collective-permute-start(bf16[16,64]{1,0:T(8,128)(2,1)S(1)} %get-tuple-element.45.refs_0_), channel_id=1, source_target_pairs={{0,8},{4,12},{8,0},{12,4},{1,9},{5,13},{9,1},{13,5},{2,10},{6,14},... | collective-permute-start | bytes 6152 | tf_op jit(solution)/shard_map/ppermute | solution.py:288
  9.4 3.2 %collective-permute-start.3 = (bf16[16,64]{1,0:T(8,128)(2,1)S(1)}, bf16[16,64]{1,0:T(8,128)(2,1)S(1)}, u32[]{:S(2)}, u32[]{:S(2)}) collective-permute-start(bf16[16,64]{1,0:T(8,128)(2,1)S(1)} %get-tuple-element.45.refs_0_), channel_id=1, source_target_pairs={{0,4},{4,0},{8,12},{12,8},{1,5},{5,1},{9,13},{13,9},{2,6},{6,2},{1... | collective-permute-start | bytes 6152 | tf_op jit(solution)/shard_map/ppermute | solution.py:288
  15.8 4.8 %collective-permute-start.6 = (bf16[16,768]{1,0:T(8,128)(2,1)S(1)}, bf16[16,768]{1,0:T(8,128)(2,1)S(1)}, u32[]{:S(2)}, u32[]{:S(2)}) collective-permute-start(bf16[16,768]{1,0:T(8,128)(2,1)S(1)} %get-tuple-element.61), channel_id=1, source_target_pairs={{0,4},{4,0},{8,12},{12,8},{1,5},{5,1},{9,13},{13,9},{2,6},{6,2},{1... | collective-permute-start | bytes 73736 | tf_op jit(solution)/shard_map/ppermute | solution.py:288
  15.9 4.7 %collective-permute-start.7 = (bf16[16,768]{1,0:T(8,128)(2,1)S(1)}, bf16[16,768]{1,0:T(8,128)(2,1)S(1)}, u32[]{:S(2)}, u32[]{:S(2)}) collective-permute-start(bf16[16,768]{1,0:T(8,128)(2,1)S(1)} %get-tuple-element.62), channel_id=1, source_target_pairs={{0,8},{4,12},{8,0},{12,4},{1,9},{5,13},{9,1},{13,5},{2,10},{6,14},... | collective-permute-start | bytes 73736 | tf_op jit(solution)/shard_map/ppermute | solution.py:288
  17.1 3.5 %collective-permute-start.8 = (bf16[16,768]{1,0:T(8,128)(2,1)S(1)}, bf16[16,768]{1,0:T(8,128)(2,1)S(1)}, u32[]{:S(2)}, u32[]{:S(2)}) collective-permute-start(bf16[16,768]{1,0:T(8,128)(2,1)S(1)} %get-tuple-element.63), channel_id=1, source_target_pairs={{0,12},{4,8},{8,4},{12,0},{1,13},{5,9},{9,5},{13,1},{2,14},{6,10},... | collective-permute-start | bytes 73736 | tf_op jit(solution)/shard_map/ppermute | solution.py:288

commit v5 on v4

--- a/solution.py
+++ b/solution.py
@@ -56,17 +56,22 @@
     copy.wait()
 
 
-def prep_kernel(count, *refs):
+def prep_kernel(count, xst_ref, bcw_ref, dtw_ref, *refs):
     src, refs = refs[:count], refs[count:]
-    (gain_ref, ngain_ref, own_ref, live_own_ref, bcw_ref, dtw_ref, bcst_ref, bcbase_ref, bctap_ref, xst_ref,
-     xbase_ref, xtap_ref, dtb_ref, rate_ref, skip_ref, live_ref) = refs[:16]
-    gain_s, ngain_s, slot_s, act_s, bccw_s, bccb_s, xcw_s, xcb_s, sems = refs[16:]
-    dst = (gain_s, ngain_s, slot_s, act_s, bcw_ref, dtw_ref, bcst_ref, bccw_s, bccb_s, xst_ref, xcw_s, xcb_s,
+    (gain_ref, ngain_ref, own_ref, live_own_ref, bcst_ref, bcbase_ref, bctap_ref,
+     xbase_ref, xtap_ref, dtb_ref, rate_ref, skip_ref, live_ref, side_ref) = refs[:14]
+    gain_s, ngain_s, slot_s, act_s, bccw_s, bccb_s, xcw_s, xcb_s, sems = refs[14:]
+    dst = (gain_s, ngain_s, slot_s, act_s, bcst_ref, bccw_s, bccb_s, xcw_s, xcb_s,
            dtb_ref, rate_ref, skip_ref)
     copies = [pltpu.make_async_copy(a, b, sems.at[i]) for i, (a, b) in enumerate(zip(src, dst))]
-    order = (2, 3, 6, 7, 8, 9, 10, 11, 0, 1, 4, 5, 12, 13, 14)
+    order = (2, 3, 4, 5, 6, 7, 8, 0, 1, 9, 10, 11)
     for i in order:
         copies[i].start()
+    side = [bcw_ref[...].astype(F32), dtw_ref[...].astype(F32)]
+    spare = side_ref.shape[1] - sum(v.shape[0] for v in side)
+    if spare:
+        side.append(jnp.zeros((spare, side_ref.shape[0]), F32))
+    side_ref[...] = jnp.concatenate(side, axis=0).T.astype(BF16)
     copies[2].wait()
     copies[3].wait()
     own = owner_mask(slot_s[...])
@@ -75,8 +80,8 @@
     own_ref[...] = own.astype(F32)
     live_own_ref[...] = (own & live).astype(BF16)
     live_ref[...] = jnp.broadcast_to(live.astype(F32), live_ref.shape)
-    for st, cw, cb, base, tap, waits in ((bcst_ref, bccw_s, bccb_s, bcbase_ref, bctap_ref, (6, 7, 8)),
-                                         (xst_ref, xcw_s, xcb_s, xbase_ref, xtap_ref, (9, 10, 11))):
+    for st, cw, cb, base, tap, waits in ((bcst_ref, bccw_s, bccb_s, bcbase_ref, bctap_ref, (4, 5, 6)),
+                                         (xst_ref, xcw_s, xcb_s, xbase_ref, xtap_ref, (7, 8))):
         for i in waits:
             copies[i].wait()
         weight = cw[...].astype(F32)
@@ -89,13 +94,13 @@
         copies[i].wait()
     gain_ref[...] = gain_s[...].reshape(1, -1)
     ngain_ref[...] = ngain_s[...].reshape(1, -1)
-    for i in (4, 5, 12, 13, 14):
+    for i in (9, 10, 11):
         copies[i].wait()
 
 
 def bc_kernel(n, *refs):
     parts, refs = refs[:n], refs[n:]
-    gain_ref, bcw_ref, dtw_ref, base_ref, tap_ref, normed_ref, bc_ref, proj_ref, dt_ref = refs
+    gain_ref, side_ref, base_ref, tap_ref, normed_ref, bc_ref, proj_ref, dt_ref = refs
     bcw, heads = bc_ref.shape[1], dt_ref.shape[1]
     me = lax.axis_index("tp")
     blocks = [p[...] for p in parts]
@@ -109,8 +114,7 @@
     inv = lax.rsqrt(jnp.mean(rows * rows, axis=1, keepdims=True) + EPS)
     normed = (rows * inv * gain_ref[...]).astype(BF16)
     normed_ref[...] = normed
-    side = jnp.concatenate([bcw_ref[...], dtw_ref[...]], axis=0)
-    both = lax.dot_general(normed, side, NT, preferred_element_type=F32).astype(BF16)
+    both = jnp.dot(normed, side_ref[...], preferred_element_type=F32).astype(BF16)
     dt_ref[...] = both[:, bcw:bcw + heads].astype(F32)
     proj = both[:, :bcw]
     proj_ref[...] = proj
@@ -304,21 +308,23 @@
     hid, = call(load_kernel, "load", (like(hidden),), [HB], (pinned(hidden),), scratch=[pltpu.SemaphoreType.DMA],
                 flops=LEAD, moved=1e5)
     parts = [hid] + spread_out([hid] * (n - 1), n)
-    src = (in_gain, norm_gain, row(pool_slot), row(active), bc_weight.T, dt_weight.T, conv_bc_state.transpose(1, 0, 2),
-           conv_bc_weight, row(conv_bc_bias), conv_x_state.transpose(1, 0, 2), conv_x_weight, conv_x_bias, row(dt_bias),
+    src = (in_gain, norm_gain, row(pool_slot), row(active), conv_bc_state.transpose(1, 0, 2),
+           conv_bc_weight, row(conv_bc_bias), conv_x_weight, conv_x_bias, row(dt_bias),
            row(log_rate), row(skip_gain))
-    held = {i: pltpu.VMEM(src[i].shape, src[i].dtype) for i in (0, 1, 2, 3, 7, 8, 10, 11)}
-    (gain, ngain, own, live_own, bcw_v, dtw_v, bcst, bcbase, bctap, xst, xbase, xtap, dtb, rate, skip, live) = call(
+    xst = conv_x_state.transpose(1, 0, 2)
+    held = {i: pltpu.VMEM(src[i].shape, src[i].dtype) for i in (0, 1, 2, 3, 5, 6, 7, 8)}
+    (gain, ngain, own, live_own, bcst, bcbase, bctap, xbase, xtap, dtb, rate, skip, live, side) = call(
         functools.partial(prep_kernel, len(src)), "prep",
-        (like(row(in_gain)), like(row(norm_gain)), sds((seqs, seqs), F32), sds((seqs, seqs), BF16), like(src[4]), like(src[5]),
-         like(src[6]), sds((seqs, bcw), F32), sds((1, bcw), F32), like(src[9]), sds((seqs, chans), F32),
-         sds((1, chans), F32), like(src[12]), like(src[13]), like(src[14]), sds((seqs, 128), F32)),
-        [HB] * len(src), tuple(map(pinned, src)), scratch=[*held.values(), pltpu.SemaphoreType.DMA((len(src),))], flops=4e6, moved=1e6)
+        (like(row(in_gain)), like(row(norm_gain)), sds((seqs, seqs), F32), sds((seqs, seqs), BF16),
+         like(src[4]), sds((seqs, bcw), F32), sds((1, bcw), F32), sds((seqs, chans), F32),
+         sds((1, chans), F32), like(src[9]), like(src[10]), like(src[11]), sds((seqs, 128), F32),
+         sds((n * width, -(-(bcw + heads) // 128) * 128), BF16)),
+        [VM] * 3 + [HB] * len(src), (xst, bc_weight.T, dt_weight.T, *map(pinned, src)), scratch=[*held.values(), pltpu.SemaphoreType.DMA((len(src),))], flops=4e6, moved=1e6)
     normed, bc_own, bcproj, dt = call(
         functools.partial(bc_kernel, n), "bc",
         (sds((seqs, n * width), BF16), sds((seqs, bcw), BF16), sds((seqs, bcw), BF16),
          sds((seqs, heads), F32)),
-        [VM] * (n + 5), (*parts, gain, bcw_v, dtw_v, bcbase, bctap), flops=4e6)
+        [VM] * (n + 4), (*parts, gain, side, bcbase, bctap), flops=4e6)
     bc_parts = [bc_own] + spread_out([bc_own] * (n - 1), n)
     wide = sds((seqs, chans), F32)
     xproj, g1, g2, g3, u, dec = call(

time: 21.5 us -> 21.5 us (level)
  no operation moved by 1% of the time
where the time goes in v5:
time: 21.5 us; the launch traced here: 21.4 us
  Pallas kernels  12.6 us (59%)
  starting transfers between devices  6.96 us (32%)
  waiting for transfers between devices  1 us (5%)
  between operations  0.82 us (4%)
    pallas_call x8, Pallas kernels, call(): pl.pallas_call(kernel, out_shape=out, in_specs=ins, out_specs=tuple(outs...  12.6 us
    ppermute x9, starting transfers between devices, spread_out(): lax.ppermute(v, 'tp', [(i, i ^ k if pairs else (i + k) % n) for i in rang...  6.96 us
    ppermute x9, waiting for transfers between devices, spread_out(): lax.ppermute(v, 'tp', [(i, i ^ k if pairs else (i + k) % n) for i in rang...  1 us
  transfers between devices with their start and end apart: 9, of which 1 were waited for; matrix products, arithmetic and copies ran while one was open for 0% of the time, Pallas kernels for 34%

profile of v5, /device:TPU:0, one launch (start us, length us, event | category | flops | bytes accessed | tf_op | source)
XLA Modules:
  0.0 21.4 jit_solution(1812197264435408228)
XLA Ops:
  0.7 0.9 %load.1.refs_0_.hid_ref = bf16[16,640]{1,0:T(8,128)(2,1)S(1)} custom-call(bf16[16,640]{1,0:T(8,128)(2,1)} %src_ref.1), custom_call_target="tpu_custom_call" | custom-call | flops 20000000000 | bytes 100000 | tf_op jit(solution)/shard_map/load/pallas_call | solution.py:269
  1.6 0.0 copy-start
  1.6 2.5 %collective-permute-start.2 = (bf16[16,640]{1,0:T(8,128)(2,1)S(1)}, bf16[16,640]{1,0:T(8,128)(2,1)S(1)}, u32[]{:S(2)}, u32[]{:S(2)}) collective-permute-start(bf16[16,640]{1,0:T(8,128)(2,1)S(1)} %load.1.refs_0_.hid_ref), channel_id=1, source_target_pairs={{0,12},{4,8},{8,4},{12,0},{1,13},{5,9},{9,5},{13,1},{2,14},{6,10},... | collective-permute-start | bytes 61448 | tf_op jit(solution)/shard_map/ppermute | solution.py:292
  4.1 0.6 %collective-permute-start.1 = (bf16[16,640]{1,0:T(8,128)(2,1)S(1)}, bf16[16,640]{1,0:T(8,128)(2,1)S(1)}, u32[]{:S(2)}, u32[]{:S(2)}) collective-permute-start(bf16[16,640]{1,0:T(8,128)(2,1)S(1)} %load.1.refs_0_.hid_ref), channel_id=1, source_target_pairs={{0,8},{4,12},{8,0},{12,4},{1,9},{5,13},{9,1},{13,5},{2,10},{6,14},... | collective-permute-start | bytes 61448 | tf_op jit(solution)/shard_map/ppermute | solution.py:292
  4.7 0.0 collective-permute-start
  4.8 2.1 %prep.1 = (f32[1,2560]{1,0:T(1,128)S(1)}, f32[1,1280]{1,0:T(1,128)S(1)}, f32[16,16]{1,0:T(8,128)S(1)}, bf16[16,16]{1,0:T(8,128)(2,1)S(1)}, bf16[3,16,64]{2,1,0:T...) custom-call(bf16[3,16,1280]{2,1,0:T(8,128)(2,1)S(1)} %bitcast.16, ...), custom_call_target="tpu_custom_call" | custom-call | flops 4000000 | bytes 1000000 | tf_op jit(solution)/shard_map/prep/pallas_call | solution.py:269
  6.9 0.0 collective-permute-done.2.refs_3_
  6.9 1.0 %collective-permute-done.1.refs_2_ = bf16[16,640]{1,0:T(8,128)(2,1)S(1)} collective-permute-done((bf16[16,640]{1,0:T(8,128)(2,1)S(1)}, bf16[16,640]{1,0:T(8,128)(2,1)S(1)}, u32[]{:S(2)}, u32[]{:S(2)}) %collective-permute-start.1) | collective-permute-done | bytes 20512 | tf_op jit(solution)/shard_map/ppermute | solution.py:292
  7.9 0.0 collective-permute-done.refs_1_
  7.9 0.4 %bc.1 = (bf16[16,2560]{1,0:T(8,128)(2,1)S(1)}, bf16[16,64]{1,0:T(8,128)(2,1)S(1)}, bf16[16,64]{1,0:T(8,128)(2,1)S(1)}, f32[16,20]{1,0:T(8,128)S(1)}) custom-call(bf16[16,640]{1,0:T(8,128)(2,1)S(1)} %load.1.refs_0_.hid_ref, bf16[16,640]{1,0:T(8,128)(2,1)S(1)} %collective-permute-done.refs_1_, bf16[16,640]{1,0:T(8,128)(2,1)S(1)} %collective-permute-done.1.refs_2_, ...), custom_call_target="tpu_custom_call" | custom-call | flops 4000000 | bytes 100000 | tf_op jit(solution)/shard_map/bc/pallas_call | solution.py:269
  8.2 0.5 %collective-permute-start.5 = (bf16[16,64]{1,0:T(8,128)(2,1)S(1)}, bf16[16,64]{1,0:T(8,128)(2,1)S(1)}, u32[]{:S(2)}, u32[]{:S(2)}) collective-permute-start(bf16[16,64]{1,0:T(8,128)(2,1)S(1)} %get-tuple-element.42.refs_0_), channel_id=1, source_target_pairs={{0,12},{4,8},{8,4},{12,0},{1,13},{5,9},{9,5},{13,1},{2,14},{6,10},... | collective-permute-start | bytes 6152 | tf_op jit(solution)/shard_map/ppermute | solution.py:292
  8.8 0.7 %collective-permute-start.4 = (bf16[16,64]{1,0:T(8,128)(2,1)S(1)}, bf16[16,64]{1,0:T(8,128)(2,1)S(1)}, u32[]{:S(2)}, u32[]{:S(2)}) collective-permute-start(bf16[16,64]{1,0:T(8,128)(2,1)S(1)} %get-tuple-element.42.refs_0_), channel_id=1, source_target_pairs={{0,8},{4,12},{8,0},{12,4},{1,9},{5,13},{9,1},{13,5},{2,10},{6,14},... | collective-permute-start | bytes 6152 | tf_op jit(solution)/shard_map/ppermute | solution.py:292
  9.4 0.7 %collective-permute-start.3 = (bf16[16,64]{1,0:T(8,128)(2,1)S(1)}, bf16[16,64]{1,0:T(8,128)(2,1)S(1)}, u32[]{:S(2)}, u32[]{:S(2)}) collective-permute-start(bf16[16,64]{1,0:T(8,128)(2,1)S(1)} %get-tuple-element.42.refs_0_), channel_id=1, source_target_pairs={{0,4},{4,0},{8,12},{12,8},{1,5},{5,1},{9,13},{13,9},{2,6},{6,2},{1... | collective-permute-start | bytes 6152 | tf_op jit(solution)/shard_map/ppermute | solution.py:292
  10.1 2.4 %proj.1 = (bf16[16,1280]{1,0:T(8,128)(2,1)S(1)}, f32[16,1280]{1,0:T(8,128)S(1)}, f32[16,1280]{1,0:T(8,128)S(1)}, f32[16,1280]{1,0:T(8,128)S(1)}, f32[1280,16]{1,0:T(8,128)S(1)}, /*index=5*/f32[16,20,128]{2,1,0:T(8,128)S(1)}) custom-call(bf16[16,2560]{1,0:T(8,128)(2,1)S(1)} %get-tuple-element.43.normed_ref, bf16[2560,1280]{1,0:T(8,128)(2,1)S(1)} %copy-done.2, ...), custom_call_target="tpu_custom_call" | custom-call | flops 1000000 | bytes 100000 | tf_op jit(solution)/shard_map/proj/pallas_call | solution.py:269
  12.6 0.0 collective-permute-done.5.refs_3_
  12.6 0.0 collective-permute-done.4.refs_2_
  12.6 3.2 %out.1 = (bf16[16,768]{1,0:T(8,128)(2,1)S(1)}, bf16[16,768]{1,0:T(8,128)(2,1)S(1)}, bf16[16,768]{1,0:T(8,128)(2,1)S(1)}, f32[16,768]{1,0:T(8,128)S(1)}, bf16[16,...) custom-call(bf16[16,64]{1,0:T(8,128)(2,1)S(1)} %get-tuple-element.42.refs_0_, ...), custom_call_target="tpu_custom_call" | custom-call | flops 200000000 | bytes 14000000 | tf_op jit(solution)/shard_map/out/pallas_call | solution.py:269
  15.8 0.1 collective-permute-start.6
  15.9 1.2 %collective-permute-start.7 = (bf16[16,768]{1,0:T(8,128)(2,1)S(1)}, bf16[16,768]{1,0:T(8,128)(2,1)S(1)}, u32[]{:S(2)}, u32[]{:S(2)}) collective-permute-start(bf16[16,768]{1,0:T(8,128)(2,1)S(1)} %get-tuple-element.59), channel_id=1, source_target_pairs={{0,8},{4,12},{8,0},{12,4},{1,9},{5,13},{9,1},{13,5},{2,10},{6,14},... | collective-permute-start | bytes 73736 | tf_op jit(solution)/shard_map/ppermute | solution.py:292
  17.1 0.7 %collective-permute-start.8 = (bf16[16,768]{1,0:T(8,128)(2,1)S(1)}, bf16[16,768]{1,0:T(8,128)(2,1)S(1)}, u32[]{:S(2)}, u32[]{:S(2)}) collective-permute-start(bf16[16,768]{1,0:T(8,128)(2,1)S(1)} %get-tuple-element.60), channel_id=1, source_target_pairs={{0,12},{4,8},{8,4},{12,0},{1,13},{5,9},{9,5},{13,1},{2,14},{6,10},... | collective-permute-start | bytes 73736 | tf_op jit(solution)/shard_map/ppermute | solution.py:292
  17.7 2.8 %state.1 = (f32[16,1280,128]{2,1,0:T(8,128)}, bf16[3,16,1280]{2,1,0:T(8,128)(2,1)}, bf16[3,16,64]{2,1,0:T(8,128)(2,1)}) custom-call(f32[16,1280,128]{2,1,0:T(8,128)} %get-tuple-element.61._, f32[16,1280,128]{2,1,0:T(8,128)S(1)} %bitcast.15, f32[1280,16]{1,0:T(8,128)S(1)} %get-tuple-element.51.after_ref.refs_11_.u_ref, ...), custom_call_target="tpu_custom_call", output_to_operand_aliasing={{0}: (0, {})} | custom-call | flops 200000000 | bytes 14000000 | tf_op jit(solution)/shard_map/state/pallas_call | solution.py:269
  20.6 0.0 collective-permute-done.7.refs_1_
  20.6 0.0 collective-permute-done.8.refs_2_
  20.6 0.8 %final.1 = bf16[16,640]{1,0:T(8,128)(2,1)} custom-call(bf16[16,640]{1,0:T(8,128)(2,1)S(1)} %load.1.refs_0_.hid_ref, f32[16,128]{1,0:T(8,128)S(1)} %get-tuple-element.37.live_ref, f32[16,768]{1,0:T(8,128)S(1)} %get-tuple-element.57.own_ref, bf16[16,768]{1,0:T(8,128)(2,1)S(1)} %collective-permute-done.6.refs_0_, ...), custom_call_target="tpu_custom_call" | custom-call | flops 1000000 | bytes 100000 | tf_op jit(solution)/shard_map/final/pallas_call | solution.py:269
  (16 shorter events, 0.0 us)
Async XLA Ops:
  0.6 4.1 %copy-start.4 = (bf16[16,3,1280]{2,0,1:T(8,128)(2,1)S(1)}, bf16[16,3,1280]{2,0,1:T(8,128)(2,1)}, u32[]{:S(2)}) copy-start(bf16[16,3,1280]{2,0,1:T(8,128)(2,1)} %param.30) | copy-start | bytes 368644
  0.6 4.1 %copy-start.6 = (bf16[2560,20]{0,1:T(8,128)(2,1)S(1)}, bf16[2560,20]{0,1:T(8,128)(2,1)}, u32[]{:S(2)}) copy-start(bf16[2560,20]{0,1:T(8,128)(2,1)} %param.25) | copy-start | bytes 307204
  0.7 4.1 %copy-start.5 = (bf16[2560,64]{0,1:T(8,128)(2,1)S(1)}, bf16[2560,64]{0,1:T(8,128)(2,1)}, u32[]{:S(2)}) copy-start(bf16[2560,64]{0,1:T(8,128)(2,1)} %param.24) | copy-start | bytes 983044
  0.7 9.5 %copy-start.2 = (bf16[2560,1280]{1,0:T(8,128)(2,1)S(1)}, bf16[2560,1280]{1,0:T(8,128)(2,1)}, u32[]{:S(2)}) copy-start(bf16[2560,1280]{1,0:T(8,128)(2,1)} %xw_ref.1) | copy-start | bytes 19660804
  0.7 9.5 %copy-start.3 = (bf16[2560,1280]{1,0:T(8,128)(2,1)S(1)}, bf16[2560,1280]{1,0:T(8,128)(2,1)}, u32[]{:S(2)}) copy-start(bf16[2560,1280]{1,0:T(8,128)(2,1)} %zw_ref.1) | copy-start | bytes 19660804
  0.7 11.9 %copy-start.1 = (bf16[1280,2560]{1,0:T(8,128)(2,1)S(1)}, bf16[1280,2560]{1,0:T(8,128)(2,1)}, u32[]{:S(2)}) copy-start(bf16[1280,2560]{1,0:T(8,128)(2,1)} %refs_10_.1) | copy-start | bytes 19660804
  1.6 11.0 %copy-start = (f32[16,20,64,128]{3,2,1,0:T(8,128)S(1)}, f32[16,20,64,128]{3,2,1,0:T(8,128)}, u32[]{:S(2)}) copy-start(f32[16,20,64,128]{3,2,1,0:T(8,128)} %param.35) | copy-start | bytes 31457284
  1.6 5.3 %collective-permute-start.2 = (bf16[16,640]{1,0:T(8,128)(2,1)S(1)}, bf16[16,640]{1,0:T(8,128)(2,1)S(1)}, u32[]{:S(2)}, u32[]{:S(2)}) collective-permute-start(bf16[16,640]{1,0:T(8,128)(2,1)S(1)} %load.1.refs_0_.hid_ref), channel_id=1, source_target_pairs={{0,12},{4,8},{8,4},{12,0},{1,13},{5,9},{9,5},{13,1},{2,14},{6,10},... | collective-permute-start | bytes 61448 | tf_op jit(solution)/shard_map/ppermute | solution.py:292
  4.1 3.8 %collective-permute-start.1 = (bf16[16,640]{1,0:T(8,128)(2,1)S(1)}, bf16[16,640]{1,0:T(8,128)(2,1)S(1)}, u32[]{:S(2)}, u32[]{:S(2)}) collective-permute-start(bf16[16,640]{1,0:T(8,128)(2,1)S(1)} %load.1.refs_0_.hid_ref), channel_id=1, source_target_pairs={{0,8},{4,12},{8,0},{12,4},{1,9},{5,13},{9,1},{13,5},{2,10},{6,14},... | collective-permute-start | bytes 61448 | tf_op jit(solution)/shard_map/ppermute | solution.py:292
  4.7 3.1 %collective-permute-start = (bf16[16,640]{1,0:T(8,128)(2,1)S(1)}, bf16[16,640]{1,0:T(8,128)(2,1)S(1)}, u32[]{:S(2)}, u32[]{:S(2)}) collective-permute-start(bf16[16,640]{1,0:T(8,128)(2,1)S(1)} %load.1.refs_0_.hid_ref), channel_id=1, source_target_pairs={{0,4},{4,0},{8,12},{12,8},{1,5},{5,1},{9,13},{13,9},{2,6},{6,2},{1... | collective-permute-start | bytes 61448 | tf_op jit(solution)/shard_map/ppermute | solution.py:292
  8.2 4.3 %collective-permute-start.5 = (bf16[16,64]{1,0:T(8,128)(2,1)S(1)}, bf16[16,64]{1,0:T(8,128)(2,1)S(1)}, u32[]{:S(2)}, u32[]{:S(2)}) collective-permute-start(bf16[16,64]{1,0:T(8,128)(2,1)S(1)} %get-tuple-element.42.refs_0_), channel_id=1, source_target_pairs={{0,12},{4,8},{8,4},{12,0},{1,13},{5,9},{9,5},{13,1},{2,14},{6,10},... | collective-permute-start | bytes 6152 | tf_op jit(solution)/shard_map/ppermute | solution.py:292
  8.8 3.8 %collective-permute-start.4 = (bf16[16,64]{1,0:T(8,128)(2,1)S(1)}, bf16[16,64]{1,0:T(8,128)(2,1)S(1)}, u32[]{:S(2)}, u32[]{:S(2)}) collective-permute-start(bf16[16,64]{1,0:T(8,128)(2,1)S(1)} %get-tuple-element.42.refs_0_), channel_id=1, source_target_pairs={{0,8},{4,12},{8,0},{12,4},{1,9},{5,13},{9,1},{13,5},{2,10},{6,14},... | collective-permute-start | bytes 6152 | tf_op jit(solution)/shard_map/ppermute | solution.py:292
  9.4 3.2 %collective-permute-start.3 = (bf16[16,64]{1,0:T(8,128)(2,1)S(1)}, bf16[16,64]{1,0:T(8,128)(2,1)S(1)}, u32[]{:S(2)}, u32[]{:S(2)}) collective-permute-start(bf16[16,64]{1,0:T(8,128)(2,1)S(1)} %get-tuple-element.42.refs_0_), channel_id=1, source_target_pairs={{0,4},{4,0},{8,12},{12,8},{1,5},{5,1},{9,13},{13,9},{2,6},{6,2},{1... | collective-permute-start | bytes 6152 | tf_op jit(solution)/shard_map/ppermute | solution.py:292
  15.8 4.8 %collective-permute-start.6 = (bf16[16,768]{1,0:T(8,128)(2,1)S(1)}, bf16[16,768]{1,0:T(8,128)(2,1)S(1)}, u32[]{:S(2)}, u32[]{:S(2)}) collective-permute-start(bf16[16,768]{1,0:T(8,128)(2,1)S(1)} %get-tuple-element.58), channel_id=1, source_target_pairs={{0,4},{4,0},{8,12},{12,8},{1,5},{5,1},{9,13},{13,9},{2,6},{6,2},{1... | collective-permute-start | bytes 73736 | tf_op jit(solution)/shard_map/ppermute | solution.py:292
  15.9 4.7 %collective-permute-start.7 = (bf16[16,768]{1,0:T(8,128)(2,1)S(1)}, bf16[16,768]{1,0:T(8,128)(2,1)S(1)}, u32[]{:S(2)}, u32[]{:S(2)}) collective-permute-start(bf16[16,768]{1,0:T(8,128)(2,1)S(1)} %get-tuple-element.59), channel_id=1, source_target_pairs={{0,8},{4,12},{8,0},{12,4},{1,9},{5,13},{9,1},{13,5},{2,10},{6,14},... | collective-permute-start | bytes 73736 | tf_op jit(solution)/shard_map/ppermute | solution.py:292
  17.1 3.5 %collective-permute-start.8 = (bf16[16,768]{1,0:T(8,128)(2,1)S(1)}, bf16[16,768]{1,0:T(8,128)(2,1)S(1)}, u32[]{:S(2)}, u32[]{:S(2)}) collective-permute-start(bf16[16,768]{1,0:T(8,128)(2,1)S(1)} %get-tuple-element.60), channel_id=1, source_target_pairs={{0,12},{4,8},{8,4},{12,0},{1,13},{5,9},{9,5},{13,1},{2,14},{6,10},... | collective-permute-start | bytes 73736 | tf_op jit(solution)/shard_map/ppermute | solution.py:292
